TPU v7x, 32 devices: a whole 2x2x4 slice. The times are simulated.
32 devices in a mesh: dp: 16 (over z, y, x), tensor: 2 (over core).
Axes of the slice: x: 2, y: 2, z: 4, core: 2. Of those that a mesh axis runs over, the one named last changes fastest.
Arguments:
- hidden_in: bfloat16 [4096, 2048], P('dp'), may hold values from -6 to 6
- norm_gain: bfloat16 [2048], P('dp'), may hold values from 0.099609375 to 1.8984375
- w_query: bfloat16 [2048, 3072], P('dp', 'tensor'), may hold values from -0.125 to 0.125
- w_latent: bfloat16 [2048, 576], P('dp'), may hold values from -0.125 to 0.125
- latent_gain: bfloat16 [512], P('dp'), may hold values from 0.099609375 to 1.8984375
- w_up: bfloat16 [512, 4096], P('dp', 'tensor'), may hold values from -0.25 to 0.25
- w_out: bfloat16 [2048, 2048], P('tensor', 'dp'), may hold values from -1 to 1
- ffn_gain: bfloat16 [2048], P('dp'), may hold values from 0.099609375 to 1.8984375
- shared_gate: bfloat16 [2048, 2816], P('dp', 'tensor'), may hold values from -0.125 to 0.125
- shared_up: bfloat16 [2048, 2816], P('dp', 'tensor'), may hold values from -0.125 to 0.125
- shared_down: bfloat16 [2816, 2048], P('tensor', 'dp'), may hold values from -0.109375 to 0.109375
- expert_gate: bfloat16 [16, 2048, 1408], P('dp', None, 'tensor'), may hold values from -0.125 to 0.125
- expert_up: bfloat16 [16, 2048, 1408], P('dp', None, 'tensor'), may hold values from -0.125 to 0.125
- expert_down: bfloat16 [16, 1408, 2048], P('dp', 'tensor'), may hold values from -0.625 to 0.625
- gate_values: float32 [4096, 6], P('dp'), may hold values from 0.05 to 0.8
- expert_ids: int32 [4096, 6], P('dp'), may hold values from 0 to 15, all different within a row; in each aligned block of 256 rows (0 to 255, 256 to 511, ...) at most 112 rows name the same one
- segment_ids: int32 [16, 256], P('dp'), may hold values from 0 to 1, never falling along the last dimension, each value on 1 to 200 neighbouring positions
- cotangent: float32 [4096, 2048], P('dp'), may hold values from -6 to 6
Outputs:
- output: bfloat16 [4096, 2048], P('dp')
- grad_input: float32 [4096, 2048], P('dp')
- grad_norm_gain: float32 [2048], P('dp')
- grad_w_query: float32 [2048, 3072], P('dp', 'tensor')
- grad_w_latent: float32 [2048, 576], P('dp')
- grad_latent_gain: float32 [512], P('dp')
- grad_w_up: float32 [512, 4096], P('dp', 'tensor')
- grad_w_out: float32 [2048, 2048], P('tensor', 'dp')
- grad_ffn_gain: float32 [2048], P('dp')
- grad_shared_gate: float32 [2048, 2816], P('dp', 'tensor')
- grad_shared_up: float32 [2048, 2816], P('dp', 'tensor')
- grad_shared_down: float32 [2816, 2048], P('tensor', 'dp')
- grad_expert_gate: float32 [16, 2048, 1408], P('dp', None, 'tensor')
- gradient_expert_upward: float32 [16, 2048, 1408], P('dp', None, 'tensor')
- grad_expert_down: float32 [16, 1408, 2048], P('dp', 'tensor')
Inputs may be any that keep to these rules, and one draw needn't show every extreme that they name: `expert_ids`: each row names 6 different experts. Within the 256 rows of one sequence no expert is named by more than 112 rows, a bound that some block reaches. `segment_ids`: along a sequence the numbers never fall; a document holds at most 200 positions.
All inputs are finite; a program needn't handle non-finite values.
Results may differ from a plain program's by a relative error of at most 0.018.
Values may be sent and summed in bfloat16 or wider, within the bound.
A program may use at most 320 MiB of HBM per device.

v0:
```python
import jax
import jax.numpy as jnp
from jax import lax
from jax.sharding import PartitionSpec as P

NOPE = 128
ROPE = 64
VDIM = 128


EPSILON = 1e-06


def rope_tables(length):
    half_width = ROPE // 2
    frequency = 10000.0 ** (-(jnp.arange(half_width, dtype=jnp.float32) * 2.0 / ROPE))
    angles = jnp.arange(length, dtype=jnp.float32)[:, None] * frequency[None, :]
    return (jnp.cos(angles), jnp.sin(angles))


def rotate(vectors, cosine, sine):
    half_width = vectors.shape[-1] // 2
    first_half = vectors[..., :half_width]
    second = vectors[..., half_width:]
    return jnp.concatenate(
        [first_half * cosine - second * sine, second * cosine + first_half * sine], axis=-1
    )


def silu_slope(gate_projected):
    sigmoid_value = jax.nn.sigmoid(gate_projected)
    return sigmoid_value * (1.0 + gate_projected * (1.0 - sigmoid_value))


def rms_forward(vectors, gain):
    inverse = lax.rsqrt(jnp.mean(vectors * vectors, axis=-1, keepdims=True) + EPSILON)
    return (vectors * inverse * gain, inverse)


def rms_backward(vectors, inverse, gain, grad_out):
    scaled = gain * grad_out
    grad_in = inverse * scaled - vectors * inverse**3 * jnp.mean(
        scaled * vectors, axis=-1, keepdims=True
    )
    return (grad_in, jnp.sum(grad_out * vectors * inverse, axis=0))


def pick_owned(
    returned_rows, flat_ids, slot_index, half_rows, core_index, length, topk_count, width
):
    owned = slot_index // half_rows == core_index
    place = jnp.where(owned, flat_ids * half_rows + slot_index - core_index * half_rows, 0)
    picked = returned_rows[place].astype(jnp.float32) * owned[:, None].astype(jnp.float32)
    return picked.reshape(length, topk_count, width)


def shards(
    hidden_in,
    norm_gain,
    w_query,
    w_latent,
    latent_gain,
    w_up,
    w_out,
    ffn_gain,
    shared_gate,
    shared_up,
    shared_down,
    expert_gate,
    expert_up,
    expert_down,
    gate_values,
    expert_ids,
    segment_ids,
    cotangent,
):
    kept = (
        lax.all_gather(norm_gain, "dp", axis=0, tiled=True),
        lax.all_gather(w_query, "dp", axis=0, tiled=True),
        lax.all_gather(w_latent, "dp", axis=0, tiled=True),
        lax.all_gather(latent_gain, "dp", axis=0, tiled=True),
        lax.all_gather(w_up, "dp", axis=0, tiled=True),
        lax.all_gather(w_out, "dp", axis=1, tiled=True),
        lax.all_gather(ffn_gain, "dp", axis=0, tiled=True),
        lax.all_gather(shared_gate, "dp", axis=0, tiled=True),
        lax.all_gather(shared_up, "dp", axis=0, tiled=True),
        lax.all_gather(shared_down, "dp", axis=1, tiled=True),
    )
    (
        full_norm,
        full_query,
        full_latent,
        full_lgain,
        full_up,
        full_out,
        full_fgain,
        full_sgate,
        full_sup,
        full_sdown,
    ) = kept
    length = hidden_in.shape[0]
    width = hidden_in.shape[1]
    topk_count = expert_ids.shape[1]
    head_count = full_query.shape[1] // (NOPE + ROPE)
    kv_rank = full_up.shape[0]
    experts_total = lax.axis_size("dp")
    capacity = max(2, 2 * (length * topk_count * 7 // (12 * experts_total)))
    cosine, sine = rope_tables(length)
    scale = (NOPE + ROPE) ** (-0.5)
    segment_row = segment_ids[0]
    position = jnp.arange(length, dtype=jnp.int32)
    allowed = (segment_row[:, None] == segment_row[None, :]) & (
        position[None, :] <= position[:, None]
    )
    tokens_f = hidden_in.astype(jnp.float32)
    normed_f, inverse_one = rms_forward(tokens_f, full_norm.astype(jnp.float32))
    normed = normed_f.astype(jnp.bfloat16)
    query_all = jnp.dot(normed, full_query, preferred_element_type=jnp.float32).reshape(
        length, head_count, NOPE + ROPE
    )
    query_rope = rotate(query_all[..., NOPE:], cosine[:, None, :], sine[:, None, :])
    queries = jnp.concatenate([query_all[..., :NOPE], query_rope], axis=-1).astype(jnp.bfloat16)
    latent_all = jnp.dot(normed, full_latent, preferred_element_type=jnp.float32)
    latent = latent_all[:, :kv_rank]
    latent_normed, latent_inverse = rms_forward(latent, full_lgain.astype(jnp.float32))
    latent_bf = latent_normed.astype(jnp.bfloat16)
    key_rope = rotate(latent_all[:, kv_rank:], cosine, sine).astype(jnp.bfloat16)
    expanded = jnp.dot(latent_bf, full_up, preferred_element_type=jnp.float32).astype(jnp.bfloat16)
    expanded = expanded.reshape(length, head_count, NOPE + VDIM)
    key_all = jnp.concatenate(
        [expanded[..., :NOPE], jnp.broadcast_to(key_rope[:, None, :], (length, head_count, ROPE))],
        axis=-1,
    )
    values = expanded[..., NOPE:]
    scores = (
        jnp.einsum("qhd,khd->hqk", queries, key_all, preferred_element_type=jnp.float32) * scale
    )
    raw_probs = jnp.where(allowed[None], jnp.exp(scores), 0.0)
    totals = jnp.sum(raw_probs, axis=-1, keepdims=True)
    log_total = jnp.log(totals)
    attn_weights = (raw_probs / totals).astype(jnp.bfloat16)
    context = jnp.einsum("hqk,khd->qhd", attn_weights, values, preferred_element_type=jnp.float32)
    context = context.reshape(length, head_count * VDIM).astype(jnp.bfloat16)
    attended_part = jnp.dot(context, full_out, preferred_element_type=jnp.float32)
    attended = lax.psum(attended_part, "tensor")
    residual = tokens_f + attended
    ffn_gain_f = full_fgain.astype(jnp.float32)
    ffn_f, inverse_two = rms_forward(residual, ffn_gain_f)
    ffn_in = ffn_f.astype(jnp.bfloat16)
    pair_count = length * topk_count
    flat_ids = expert_ids.reshape(-1)
    onehot = (flat_ids[:, None] == jnp.arange(experts_total, dtype=jnp.int32)[None, :]).astype(
        jnp.int32
    )
    earlier = jnp.cumsum(onehot, axis=0) - onehot
    slot_index = jnp.sum(earlier * onehot, axis=1)
    target = flat_ids * capacity + slot_index
    pair_of_slot = (
        jnp.full((experts_total * capacity,), pair_count, jnp.int32)
        .at[target]
        .set(jnp.arange(pair_count, dtype=jnp.int32))
    )
    token_of_slot = pair_of_slot // topk_count
    ffn_padded = jnp.concatenate([ffn_in, jnp.zeros((1, width), jnp.bfloat16)], axis=0)
    outgoing = ffn_padded[token_of_slot].reshape(experts_total, capacity, width)
    cot_bf = cotangent.astype(jnp.bfloat16)
    grad_rows = (
        (gate_values[:, :, None] * cotangent[:, None, :])
        .astype(jnp.bfloat16)
        .reshape(pair_count, width)
    )
    grad_padded = jnp.concatenate([grad_rows, jnp.zeros((1, width), jnp.bfloat16)], axis=0)
    grad_outgoing = grad_padded[pair_of_slot].reshape(experts_total, capacity, width)
    half_rows = capacity // lax.axis_size("tensor")
    core_index = lax.axis_index("tensor")
    portion = lax.dynamic_slice_in_dim(outgoing, core_index * half_rows, half_rows, 1)
    grad_portion = lax.dynamic_slice_in_dim(grad_outgoing, core_index * half_rows, half_rows, 1)
    arrived_half, grad_half = (
        lax.all_to_all(portion, "dp", split_axis=0, concat_axis=0, tiled=True),
        lax.all_to_all(grad_portion, "dp", split_axis=0, concat_axis=0, tiled=True),
    )
    arrived, grad_arrived = (
        lax.all_gather(arrived_half, "tensor", axis=1, tiled=True),
        lax.all_gather(grad_half, "tensor", axis=1, tiled=True),
    )
    rows_per_expert = arrived.reshape(-1, width)
    grad_arrived = grad_arrived.reshape(-1, width)
    local_gate = expert_gate[0]
    resident_up_weight = expert_up[0]
    local_down = expert_down[0]
    gate_projected = jnp.dot(rows_per_expert, local_gate, preferred_element_type=jnp.float32)
    up_proj = jnp.dot(rows_per_expert, resident_up_weight, preferred_element_type=jnp.float32)
    expert_hidden = (jax.nn.silu(gate_projected) * up_proj).astype(jnp.bfloat16)
    expert_part = jnp.dot(expert_hidden, local_down, preferred_element_type=jnp.float32)
    shared_gproj = jnp.dot(ffn_in, full_sgate, preferred_element_type=jnp.float32)
    shared_uproj = jnp.dot(ffn_in, full_sup, preferred_element_type=jnp.float32)
    shared_hidden = (jax.nn.silu(shared_gproj) * shared_uproj).astype(jnp.bfloat16)
    shared_part = jnp.dot(shared_hidden, full_sdown, preferred_element_type=jnp.float32)
    expert_half = lax.psum_scatter(
        expert_part.reshape(experts_total, capacity, width),
        "tensor",
        scatter_dimension=1,
        tiled=True,
    )
    returned_half = lax.all_to_all(
        expert_half.astype(jnp.bfloat16), "dp", split_axis=0, concat_axis=0, tiled=True
    ).reshape(-1, width)
    picked = pick_owned(
        returned_half, flat_ids, slot_index, half_rows, core_index, length, topk_count, width
    )
    routed_part = jnp.sum(picked * gate_values[:, :, None], axis=1)
    ffn_total = lax.psum(shared_part + routed_part, "tensor")
    output = (residual + ffn_total).astype(jnp.bfloat16)
    expert_hidden_gradient = jnp.dot(grad_arrived, local_down.T, preferred_element_type=jnp.float32)
    expert_gate_gradient = (expert_hidden_gradient * up_proj * silu_slope(gate_projected)).astype(
        jnp.bfloat16
    )
    expert_up_gradient = (expert_hidden_gradient * jax.nn.silu(gate_projected)).astype(jnp.bfloat16)
    grad_expert_down = jnp.dot(expert_hidden.T, grad_arrived, preferred_element_type=jnp.float32)
    grad_expert_gate = jnp.dot(
        rows_per_expert.T, expert_gate_gradient, preferred_element_type=jnp.float32
    )
    gradient_expert_upward = jnp.dot(
        rows_per_expert.T, expert_up_gradient, preferred_element_type=jnp.float32
    )
    expert_back_part = jnp.dot(
        expert_gate_gradient, local_gate.T, preferred_element_type=jnp.float32
    ) + jnp.dot(expert_up_gradient, resident_up_weight.T, preferred_element_type=jnp.float32)
    grad_shidden = jnp.dot(cot_bf, full_sdown.T, preferred_element_type=jnp.float32)
    grad_sgate = (grad_shidden * shared_uproj * silu_slope(shared_gproj)).astype(jnp.bfloat16)
    grad_sup = (grad_shidden * jax.nn.silu(shared_gproj)).astype(jnp.bfloat16)
    g_sdown = jnp.dot(shared_hidden.T, cot_bf, preferred_element_type=jnp.float32)
    g_sgate = jnp.dot(ffn_in.T, grad_sgate, preferred_element_type=jnp.float32)
    g_sup = jnp.dot(ffn_in.T, grad_sup, preferred_element_type=jnp.float32)
    shared_back_part = jnp.dot(
        grad_sgate, full_sgate.T, preferred_element_type=jnp.float32
    ) + jnp.dot(grad_sup, full_sup.T, preferred_element_type=jnp.float32)
    back_half = lax.psum_scatter(
        expert_back_part.reshape(experts_total, capacity, width),
        "tensor",
        scatter_dimension=1,
        tiled=True,
    )
    back_returned_half = lax.all_to_all(
        back_half.astype(jnp.bfloat16), "dp", split_axis=0, concat_axis=0, tiled=True
    ).reshape(-1, width)
    back_picked = pick_owned(
        back_returned_half, flat_ids, slot_index, half_rows, core_index, length, topk_count, width
    )
    grad_ffn = lax.psum(shared_back_part + jnp.sum(back_picked, axis=1), "tensor")
    grad_res_part, g_fgain = rms_backward(residual, inverse_two, ffn_gain_f, grad_ffn)
    grad_residual = cotangent + grad_res_part
    grad_attn = grad_residual.astype(jnp.bfloat16)
    g_out = jnp.dot(context.T, grad_attn, preferred_element_type=jnp.float32)
    grad_context = (
        jnp.dot(grad_attn, full_out.T, preferred_element_type=jnp.float32)
        .astype(jnp.bfloat16)
        .reshape(length, head_count, VDIM)
    )
    probs = jnp.where(allowed[None], jnp.exp(scores - log_total), 0.0)
    weights_back = probs.astype(jnp.bfloat16)
    grad_values = jnp.einsum(
        "hqk,qhd->khd", weights_back, grad_context, preferred_element_type=jnp.float32
    )
    grad_weights = jnp.einsum(
        "qhd,khd->hqk", grad_context, values, preferred_element_type=jnp.float32
    )
    row_delta = jnp.sum(probs * grad_weights, axis=-1, keepdims=True)
    grad_scores = (probs * (grad_weights - row_delta) * scale).astype(jnp.bfloat16)
    grad_queries = jnp.einsum(
        "hqk,khd->qhd", grad_scores, key_all, preferred_element_type=jnp.float32
    )
    grad_keys = jnp.einsum("hqk,qhd->khd", grad_scores, queries, preferred_element_type=jnp.float32)
    grad_qrope = rotate(grad_queries[..., NOPE:], cosine[:, None, :], -sine[:, None, :])
    grad_query_all = (
        jnp.concatenate([grad_queries[..., :NOPE], grad_qrope], axis=-1)
        .reshape(length, head_count * (NOPE + ROPE))
        .astype(jnp.bfloat16)
    )
    grad_expanded = (
        jnp.concatenate([grad_keys[..., :NOPE], grad_values], axis=-1)
        .reshape(length, head_count * (NOPE + VDIM))
        .astype(jnp.bfloat16)
    )
    g_up = jnp.dot(latent_bf.T, grad_expanded, preferred_element_type=jnp.float32)
    g_query = jnp.dot(normed.T, grad_query_all, preferred_element_type=jnp.float32)
    latent_part = jnp.dot(grad_expanded, full_up.T, preferred_element_type=jnp.float32)
    rope_part = rotate(jnp.sum(grad_keys[..., NOPE:], axis=1), cosine, -sine)
    grad_latent_normed, grad_key_rope = lax.psum((latent_part, rope_part), "tensor")
    grad_latent, g_lgain = rms_backward(
        latent, latent_inverse, full_lgain.astype(jnp.float32), grad_latent_normed
    )
    grad_latent_all = jnp.concatenate([grad_latent, grad_key_rope], axis=-1).astype(jnp.bfloat16)
    g_latent = jnp.dot(normed.T, grad_latent_all, preferred_element_type=jnp.float32)
    input_part = jnp.dot(grad_query_all, full_query.T, preferred_element_type=jnp.float32)
    grad_normed = lax.psum(input_part, "tensor") + jnp.dot(
        grad_latent_all, full_latent.T, preferred_element_type=jnp.float32
    )
    grad_in_part, g_norm = rms_backward(
        tokens_f, inverse_one, full_norm.astype(jnp.float32), grad_normed
    )
    grad_input = grad_residual + grad_in_part
    summed = (
        lax.psum_scatter(g_norm, "dp", scatter_dimension=0, tiled=True),
        lax.psum_scatter(g_query, "dp", scatter_dimension=0, tiled=True),
        lax.psum_scatter(g_latent, "dp", scatter_dimension=0, tiled=True),
        lax.psum_scatter(g_lgain, "dp", scatter_dimension=0, tiled=True),
        lax.psum_scatter(g_up, "dp", scatter_dimension=0, tiled=True),
        lax.psum_scatter(g_out, "dp", scatter_dimension=1, tiled=True),
        lax.psum_scatter(g_fgain, "dp", scatter_dimension=0, tiled=True),
        lax.psum_scatter(g_sgate, "dp", scatter_dimension=0, tiled=True),
        lax.psum_scatter(g_sup, "dp", scatter_dimension=0, tiled=True),
        lax.psum_scatter(g_sdown, "dp", scatter_dimension=1, tiled=True),
    )
    s_norm, s_query, s_latent, s_lgain, s_up, s_out, s_fgain, s_sgate, s_sup, s_sdown = summed
    return (
        output,
        grad_input,
        s_norm,
        s_query,
        s_latent,
        s_lgain,
        s_up,
        s_out,
        s_fgain,
        s_sgate,
        s_sup,
        s_sdown,
        grad_expert_gate[None],
        gradient_expert_upward[None],
        grad_expert_down[None],
    )


def solution(mesh):
    in_specs = (
        P("dp", None),
        P("dp"),
        P("dp", "tensor"),
        P("dp", None),
        P("dp"),
        P("dp", "tensor"),
        P("tensor", "dp"),
        P("dp"),
        P("dp", "tensor"),
        P("dp", "tensor"),
        P("tensor", "dp"),
        P("dp", None, "tensor"),
        P("dp", None, "tensor"),
        P("dp", "tensor", None),
        P("dp", None),
        P("dp", None),
        P("dp", None),
        P("dp", None),
    )
    out_specs = (
        P("dp", None),
        P("dp", None),
        P("dp"),
        P("dp", "tensor"),
        P("dp", None),
        P("dp"),
        P("dp", "tensor"),
        P("tensor", "dp"),
        P("dp"),
        P("dp", "tensor"),
        P("dp", "tensor"),
        P("tensor", "dp"),
        P("dp", None, "tensor"),
        P("dp", None, "tensor"),
        P("dp", "tensor", None),
    )
    return jax.shard_map(shards, mesh=mesh, in_specs=in_specs, out_specs=out_specs, check_vma=False)
```

profile of v0, /device:TPU:0, one launch (start us, length us, event | category | flops | bytes accessed | tf_op | source)
XLA Modules:
  0.0 2568.7 jit_solution(14355610848049285387)
XLA Ops:
  11.1 4.6 reduce-window.6
  17.9 9.8 mul.571
  27.7 15.8 mul.572
  43.4 8.0 multiply_convert_fusion
  51.4 6.6 concatenate.40
  59.4 6.2 scatter_custom_fusion
  66.3 18.2 gather_fusion.2
  84.5 4.4 constant_dynamic-slice_fusion
  88.8 8.6 all-to-all-start.2
  97.5 111.0 %all-gather = bf16[16,1,128]{2,1,0:T(2,128)(2,1)S(1)} all-gather(bf16[1,1,128]{2,1,0:T(2,128)(2,1)S(1)} %bitcast.144), channel_id=1, replica_groups=mesh['dp'=16,'tensor'=2] {'dp'}, dimensions={0}, use_global_device_ids=true | all-gather | bytes 4352 | tf_op jit(solution)/shard_map/all_gather | solution.py:78
  210.1 50.3 %all-reduce.2 = bf16[512]{0:T(512)(128)(2,1)S(1)} all-reduce(bf16[512]{0:T(512)(128)(2,1)S(1)} %dynamic-update-slice), channel_id=1, replica_groups=mesh['dp'=16,'tensor'=2] {'dp'}, use_global_device_ids=true, to_apply=%add.2 | all-reduce | flops 512 | bytes 2048
  274.7 5.9 all-gather.16.cloned.1.call-done
  280.6 5.8 fusion.94
  290.4 80.0 %all-gather.18.cloned.1.call-done = bf16[1024,2048]{1,0:T(8,128)(2,1)} async-done(((bf16[1024,128]{1,0:T(8,128)(2,1)}), bf16[1024,2048]{1,0:T(8,128)(2,1)}) %all-gather.18.cloned.1.call-update) | async-done | bytes 4194320 | tf_op jit(solution)/shard_map/all_gather | solution.py:83
  370.5 4.8 fusion.99
  375.9 37.8 %all-gather.1 = bf16[16,1,128]{2,1,0:T(2,128)(2,1)S(1)} all-gather(bf16[1,1,128]{2,1,0:T(2,128)(2,1)S(1)} %bitcast.145), channel_id=1, replica_groups=mesh['dp'=16,'tensor'=2] {'dp'}, dimensions={0}, use_global_device_ids=true | all-gather | bytes 4352 | tf_op jit(solution)/shard_map/all_gather | solution.py:84
  419.1 16.2 gather_fusion
  437.7 78.8 %all_to_all.20 = bf16[16,56,2048]{2,1,0:T(8,128)(2,1)} all-to-all(bf16[16,56,2048]{2,1,0:T(8,128)(2,1)S(1)} %constant_dynamic-slice_fusion.1), channel_id=1, replica_groups=mesh['dp'=16,'tensor'=2] {'dp'}, dimensions={0} | all-to-all | bytes 7340032 | tf_op jit(solution)/shard_map/all_to_all | solution.py:179
  516.8 10.6 fusion.4
  527.4 6.1 all-gather.26.cloned.1.call-done
  533.5 10.8 fusion.11
  544.4 10.4 multiply_convert_fusion.3
  554.7 9.2 fusion.9
  564.0 12.5 convolution_add_fusion
  579.9 14.4 fusion.2
  598.9 5.5 convert_element_type.156
  604.4 6.9 all-to-all-start.3
  611.9 11.7 reduce-scatter.10.cloned.1.call-done
  623.6 5.5 convert_element_type.145
  629.1 74.3 %all-to-all-done.3 = bf16[16,56,2048]{2,1,0:T(8,128)(2,1)} async-done(((bf16[16,56,2048]{2,1,0:T(8,128)(2,1)}), bf16[16,56,2048]{2,1,0:T(8,128)(2,1)}, u32[]{:S(2)}, u32[]{:S(2)}) %all-to-all-start.3) | async-done | bytes 3670048 | tf_op jit(solution)/shard_map/all_to_all | solution.py:244
  703.3 22.7 all-to-all-start.1
  726.5 73.1 %all-gather.20.cloned.1.call-done = bf16[2048,1408]{1,0:T(8,128)(2,1)} async-done(((bf16[128,1408]{1,0:T(8,128)(2,1)}), bf16[2048,1408]{1,0:T(8,128)(2,1)}) %all-gather.20.cloned.1.call-update) | async-done | bytes 5767184 | tf_op jit(solution)/shard_map/all_gather | solution.py:85
  799.6 5.5 fusion.100
  805.1 88.9 %all-gather.22.cloned.1.call-done = bf16[2048,1408]{1,0:T(8,128)(2,1)} async-done(((bf16[128,1408]{1,0:T(8,128)(2,1)}), bf16[2048,1408]{1,0:T(8,128)(2,1)}) %all-gather.22.cloned.1.call-update) | async-done | bytes 5767184 | tf_op jit(solution)/shard_map/all_gather | solution.py:86
  894.0 5.5 fusion.101
  899.6 104.0 %all-gather.24.cloned.1.call-done = bf16[1408,2048]{1,0:T(8,128)(2,1)} async-done(((bf16[1408,128]{1,0:T(8,128)(2,1)}), bf16[1408,2048]{1,0:T(8,128)(2,1)}) %all-gather.24.cloned.1.call-update) | async-done | bytes 5767184 | tf_op jit(solution)/shard_map/all_gather | solution.py:87
  1003.6 7.3 multiply_convert_fusion.6
  1014.0 15.6 gather_fusion.3
  1029.7 11.7 reshape.403
  1041.3 15.2 gather_fusion.1
  1056.6 11.7 reshape.402
  1068.3 18.2 multiply_reduce_fusion
  1086.5 5.9 fusion.13
  1093.5 6.8 convolution_add_fusion.3
  1100.3 11.7 all-reduce.14.cloned.1.call-done
  1123.8 6.2 fusion.36
  1132.4 6.1 fusion.33
  1143.3 6.0 fusion.103
  1150.4 7.7 fusion.104
  1159.2 7.6 fusion.105
  1167.9 8.3 fusion.49
  1193.2 6.1 fusion.46
  1200.4 7.8 fusion.92
  1209.5 10.1 convolution_bitcast_fusion.2
  1219.6 10.4 convolution_bitcast_fusion
  1230.1 7.1 convolution_bitcast_fusion.1
  1239.9 78.2 %all-reduce.6 = (f32[2048]{0:T(1024)S(1)}, f32[512]{0:T(512)S(1)}, f32[2048]{0:T(1024)S(1)}) all-reduce(f32[2048]{0:T(1024)S(1)} %get-tuple-element.17, f32[512]{0:T(512)S(1)} %get-tuple-element.19, f32[2048]{0:T(1024)S(1)} %get-tuple-element.15), channel_id=4, replica_groups=mesh['dp'=16,'tensor'=2] {'dp'}, use_global_device_ids=true, to_apply=%region_24.25.clone | all-reduce | flops 4608 | bytes 36864
  1325.4 102.0 %reduce-scatter.22.cloned.1.call-done = f32[128,1408]{1,0:T(8,128)} async-done(((f32[2048,1408]{1,0:T(8,128)}), f32[128,1408]{1,0:T(8,128)}) %reduce-scatter.22.cloned.1.call-update) | async-done | bytes 720912 | tf_op jit(solution)/shard_map/reduce_scatter | solution.py:311
  1427.4 248.3 %reduce-scatter.24.cloned.1.call-done = f32[128,1408]{1,0:T(8,128)} async-done(((f32[2048,1408]{1,0:T(8,128)}), f32[128,1408]{1,0:T(8,128)}) %reduce-scatter.24.cloned.1.call-update) | async-done | bytes 720912 | tf_op jit(solution)/shard_map/reduce_scatter | solution.py:312
  1675.7 248.4 %reduce-scatter.26.cloned.1.call-done = f32[1408,128]{1,0:T(8,128)} async-done(((f32[1408,2048]{1,0:T(8,128)}), f32[1408,128]{1,0:T(8,128)}) %reduce-scatter.26.cloned.1.call-update) | async-done | bytes 720912 | tf_op jit(solution)/shard_map/reduce_scatter | solution.py:313
  1924.1 102.7 %reduce-scatter.18.cloned.1.call-done = f32[32,2048]{1,0:T(8,128)} async-done(((f32[512,2048]{1,0:T(8,128)}), f32[32,2048]{1,0:T(8,128)}) %reduce-scatter.18.cloned.1.call-update) | async-done | bytes 262160 | tf_op jit(solution)/shard_map/reduce_scatter | solution.py:308
  2026.7 143.7 %reduce-scatter.16.cloned.1.call-done = f32[128,576]{0,1:T(8,128)} async-done(((f32[2048,576]{0,1:T(8,128)}), f32[128,576]{0,1:T(8,128)}) %reduce-scatter.16.cloned.1.call-update) | async-done | bytes 294928 | tf_op jit(solution)/shard_map/reduce_scatter | solution.py:306
  2170.5 179.5 %reduce-scatter.20.cloned.1.call-done = f32[1024,128]{1,0:T(8,128)} async-done(((f32[1024,2048]{1,0:T(8,128)}), f32[1024,128]{1,0:T(8,128)}) %reduce-scatter.20.cloned.1.call-update) | async-done | bytes 524304 | tf_op jit(solution)/shard_map/reduce_scatter | solution.py:309
  2350.0 211.4 %reduce-scatter.14.cloned.1.call-done = f32[128,1536]{1,0:T(8,128)} async-done(((f32[2048,1536]{1,0:T(8,128)}), f32[128,1536]{1,0:T(8,128)}) %reduce-scatter.14.cloned.1.call-update) | async-done | bytes 786448 | tf_op jit(solution)/shard_map/reduce_scatter | solution.py:305
  (312 shorter events, 98.8 us)
Async XLA Ops:
  7.2 537.2 %copy-start = (bf16[1,2048,704]{1,2,0:T(8,128)(2,1)S(1)}, bf16[1,2048,704]{1,2,0:T(8,128)(2,1)}, u32[]{:S(2)}) copy-start(bf16[1,2048,704]{1,2,0:T(8,128)(2,1)} %param.30) | copy-start | bytes 8650756
  7.2 10.4 copy-start.62
  7.2 256.1 %all-gather.12.cloned.1.call-start = ((), (), s32[]{:S(2)}) async-start(), calls=%async_computation.13 | async-start | bytes 2506752 | tf_op jit(solution)/shard_map/all_gather | solution.py:80
  7.9 259.0 %all-gather.14.cloned.1.call-start = ((), (), s32[]{:S(2)}) async-start(), calls=%async_computation.14 | async-start | bytes 2228224 | tf_op jit(solution)/shard_map/all_gather | solution.py:82
  8.7 271.9 %all-gather.16.cloned.1.call-start = ((), (), s32[]{:S(2)}) async-start(), calls=%async_computation.15 | async-start | bytes 6684672 | tf_op jit(solution)/shard_map/all_gather | solution.py:79
  9.4 361.0 %all-gather.18.cloned.1.call-start = ((), (), s32[]{:S(2)}) async-start(), calls=%async_computation.16 | async-start | bytes 4456448 | tf_op jit(solution)/shard_map/all_gather | solution.py:83
  17.7 9.9 copy-start.25
  88.8 8.7 copy-start.72
  88.8 119.8 %copy-start.71 = (u32[32]{0:T(128)S(1)}, u32[32]{0:T(128)}, u32[]{:S(2)}) copy-start(u32[32]{0:T(128)} %constant.90) | copy-start | bytes 388
  88.8 121.0 %copy-start.78 = (bf16[32]{0:T(256)(128)(2,1)S(1)}, bf16[32]{0:T(256)(128)(2,1)}, u32[]{:S(2)}) copy-start(bf16[32]{0:T(256)(128)(2,1)} %param.22) | copy-start | bytes 196
  88.8 173.7 %copy-start.67 = (s32[1,256]{1,0:T(1,128)S(1)}, s32[1,256]{1,0:T(1,128)}, u32[]{:S(2)}) copy-start(s32[1,256]{1,0:T(1,128)} %param.34) | copy-start | bytes 3076
  88.8 324.9 %all-to-all-start.2 = ((bf16[16,56,2048]{2,1,0:T(8,128)(2,1)}), bf16[16,56,2048]{2,1,0:T(8,128)(2,1)}, u32[]{:S(2)}, u32[]{:S(2)}) async-start(bf16[16,56,2048]{2,1,0:T(8,128)(2,1)} %constant_dynamic-slice_fusion), calls=%async_computation.3 | async-start | bytes 7340032 | tf_op jit(solution)/shard_map/all_to_all | solution.py:180
  97.4 316.4 %all-reduce.12.cloned.1.call-start = ((), (), s32[]{:S(2)}) async-start(), calls=%async_computation.17 | async-start | bytes 4194304 | tf_op jit(solution)/shard_map/psum | solution.py:145
  208.6 72.0 %copy-start.37 = (f32[16,1,128]{2,1,0:T(1,128)}, f32[16,1,128]{2,1,0:T(1,128)S(1)}, u32[]{:S(2)}) copy-start(f32[16,1,128]{2,1,0:T(1,128)S(1)} %convert_element_type.167) | copy-start | bytes 24580
  260.4 14.0 copy-start.69
  262.6 18.0 copy-start.50
  266.2 8.3 copy-start.11
  274.7 11.9 copy-start.39
  290.4 84.8 %copy-start.29 = (bf16[8,128,256]{2,1,0:T(8,128)(2,1)}, bf16[8,128,256]{2,1,0:T(8,128)(2,1)S(1)}, u32[]{:S(2)}) copy-start(bf16[8,128,256]{2,1,0:T(8,128)(2,1)S(1)} %convolution_convert_fusion.2) | copy-start | bytes 1572868
  375.3 141.5 %all-gather.28.cloned.1.call-start = ((), (), s32[]{:S(2)}) async-start(), calls=%async_computation.23 | async-start | bytes 11010048 | tf_op jit(solution)/shard_map/all_gather | solution.py:184
  413.8 119.8 %all-gather.26.cloned.1.call-start = ((), (), s32[]{:S(2)}) async-start(), calls=%async_computation.21 | async-start | bytes 11010048 | tf_op jit(solution)/shard_map/all_gather | solution.py:183
  516.6 82.4 %reduce-scatter.12.cloned.1.call-start = ((), (), s32[]{:S(2)}) async-start(), calls=%async_computation.24 | async-start | bytes 22020096 | tf_op jit(solution)/shard_map/reduce_scatter | solution.py:238
  533.5 10.8 copy-start.74
  533.5 10.8 copy-start.83
  544.4 10.4 copy-start.77
  554.7 9.2 copy-start.84
  554.7 9.2 copy-start.81
  576.5 47.1 %reduce-scatter.10.cloned.1.call-start = ((), (), s32[]{:S(2)}) async-start(), calls=%async_computation.22 | async-start | bytes 22020096 | tf_op jit(solution)/shard_map/reduce_scatter | solution.py:199
  594.3 205.3 %all-gather.20.cloned.1.call-start = ((), (), s32[]{:S(2)}) async-start(), calls=%async_computation.18 | async-start | bytes 6127616 | tf_op jit(solution)/shard_map/all_gather | solution.py:85
  594.9 299.1 %all-gather.22.cloned.1.call-start = ((), (), s32[]{:S(2)}) async-start(), calls=%async_computation.19 | async-start | bytes 6127616 | tf_op jit(solution)/shard_map/all_gather | solution.py:86
  604.4 98.9 %all-to-all-start.3 = ((bf16[16,56,2048]{2,1,0:T(8,128)(2,1)}), bf16[16,56,2048]{2,1,0:T(8,128)(2,1)}, u32[]{:S(2)}, u32[]{:S(2)}) async-start(bf16[16,56,2048]{2,1,0:T(8,128)(2,1)} %convert_element_type.156), calls=%async_computation.5 | async-start | bytes 7340032 | tf_op jit(solution)/shard_map/all_to_all | solution.py:244
  611.3 392.3 %all-gather.24.cloned.1.call-start = ((), (), s32[]{:S(2)}) async-start(), calls=%async_computation.20 | async-start | bytes 6127616 | tf_op jit(solution)/shard_map/all_gather | solution.py:87
  629.1 97.0 %copy-start.43 = (s32[1536]{0:T(1024)S(1)}, s32[1536]{0:T(1024)}, u32[]{:S(2)}) copy-start(s32[1536]{0:T(1024)} %copy-done.42) | copy-start | bytes 18436
  629.1 97.4 %copy-start.59 = (s32[1536]{0:T(1024)S(1)}, s32[1536]{0:T(1024)}, u32[]{:S(2)}) copy-start(s32[1536]{0:T(1024)} %get-tuple-element.23) | copy-start | bytes 18436
  629.1 170.5 %copy-start.7 = (bf16[256,2048]{1,0:T(8,128)(2,1)S(1)}, bf16[256,2048]{1,0:T(8,128)(2,1)}, u32[]{:S(2)}) copy-start(bf16[256,2048]{1,0:T(8,128)(2,1)} %copy-done.6) | copy-start | bytes 3145732
  703.3 338.0 %all-to-all-start.1 = ((bf16[16,56,2048]{2,1,0:T(8,128)(2,1)}), bf16[16,56,2048]{2,1,0:T(8,128)(2,1)}, u32[]{:S(2)}, u32[]{:S(2)}) async-start(bf16[16,56,2048]{2,1,0:T(8,128)(2,1)} %convert_element_type.145), calls=%async_computation.2 | async-start | bytes 7340032 | tf_op jit(solution)/shard_map/all_to_all | solution.py:205
  726.0 386.0 %all-reduce.14.cloned.1.call-start = ((), (), s32[]{:S(2)}) async-start(), calls=%async_computation.25 | async-start | bytes 4194304 | tf_op jit(solution)/shard_map/psum | solution.py:250
  1003.6 7.3 copy-start.75
  1010.9 75.6 %copy-start.19 = (bf16[256,1408]{1,0:T(8,128)(2,1)}, bf16[256,1408]{1,0:T(8,128)(2,1)S(1)}, u32[]{:S(2)}) copy-start(bf16[256,1408]{1,0:T(8,128)(2,1)S(1)} %get-tuple-element.36) | copy-start | bytes 2162692
  1056.6 11.7 copy-start.26
  1068.3 18.2 copy-start.23
  1092.4 92.9 %all-reduce.16.cloned.1.call-start = ((), (), s32[]{:S(2)}) async-start(), calls=%async_computation.33 | async-start | bytes 9437184 | tf_op jit(solution)/shard_map/psum | solution.py:212
  1093.5 18.6 copy-start.3
  1093.5 18.6 copy-start.49
  1093.5 18.6 copy-start.61
  1100.3 14.1 copy-start.66
  1123.8 8.6 copy-start.34
  1132.4 7.6 copy-start.40
  1141.5 7.8 copy-start.17
  1149.3 278.1 %reduce-scatter.22.cloned.1.call-start = ((), (), s32[]{:S(2)}) async-start(), calls=%async_computation.30 | async-start | bytes 12255232 | tf_op jit(solution)/shard_map/reduce_scatter | solution.py:311
  1158.1 517.6 %reduce-scatter.24.cloned.1.call-start = ((), (), s32[]{:S(2)}) async-start(), calls=%async_computation.31 | async-start | bytes 12255232 | tf_op jit(solution)/shard_map/reduce_scatter | solution.py:312
  1166.8 757.3 %reduce-scatter.26.cloned.1.call-start = ((), (), s32[]{:S(2)}) async-start(), calls=%async_computation.32 | async-start | bytes 12255232 | tf_op jit(solution)/shard_map/reduce_scatter | solution.py:313
  1176.3 850.5 %reduce-scatter.18.cloned.1.call-start = ((), (), s32[]{:S(2)}) async-start(), calls=%async_computation.28 | async-start | bytes 4456448 | tf_op jit(solution)/shard_map/reduce_scatter | solution.py:308
  1181.6 988.9 %reduce-scatter.16.cloned.1.call-start = ((), (), s32[]{:S(2)}) async-start(), calls=%async_computation.27 | async-start | bytes 5013504 | tf_op jit(solution)/shard_map/reduce_scatter | solution.py:306
  1192.2 1157.9 %reduce-scatter.20.cloned.1.call-start = ((), (), s32[]{:S(2)}) async-start(), calls=%async_computation.29 | async-start | bytes 8912896 | tf_op jit(solution)/shard_map/reduce_scatter | solution.py:309
  1199.3 1362.2 %reduce-scatter.14.cloned.1.call-start = ((), (), s32[]{:S(2)}) async-start(), calls=%async_computation.26 | async-start | bytes 13369344 | tf_op jit(solution)/shard_map/reduce_scatter | solution.py:305
  1209.5 10.1 copy-start.82
  1209.5 20.5 slice-start
  1219.6 10.4 slice-start.1
  1219.6 10.4 copy-start.85
  1230.0 7.2 copy-start.4
  1230.0 7.2 copy-start.21
  1230.0 7.2 copy-start.22
  1322.8 1238.6 %copy-start.1 = (bf16[1,2048,704]{1,2,0:T(8,128)(2,1)S(1)}, bf16[1,2048,704]{1,2,0:T(8,128)(2,1)}, u32[]{:S(2)}) copy-start(bf16[1,2048,704]{1,2,0:T(8,128)(2,1)} %param.30) | copy-start | bytes 8650756
  (48 other events, 113.3 us)
Sparse Core Ops, SparseCore 0:
  10.7 69.0 all-gather.11
  82.6 103.0 all-gather.13
  188.5 92.0 all-gather.15
  283.1 87.2 all-gather.17
  375.4 19.4 all-reduce.11
  413.9 14.1 all-gather.27
  516.7 16.8 all-gather.25
  576.6 22.2 reduce-scatter.11
  601.2 22.3 reduce-scatter.9
  626.1 173.4 all-gather.19
  802.3 91.6 all-gather.21
  896.6 106.9 all-gather.23
  1092.5 19.4 all-reduce.13
  1149.4 30.3 all-reduce.15
  1182.6 244.7 reduce-scatter.21
  1430.1 245.5 reduce-scatter.23
  1678.4 245.5 reduce-scatter.25
  1926.8 99.8 reduce-scatter.17
  2032.5 137.9 reduce-scatter.15
  2173.2 176.7 reduce-scatter.19
  2356.2 205.1 reduce-scatter.13
where the time goes:
time: 2580 us; the launch traced here: 2570 us
  waiting for transfers between devices  1700 us (66%)
  blocking collectives  360 us (14%)
  matrix products  222 us (9%)
  local copies, waits for them, and re-layouts  165 us (6%)
  other arithmetic  64 us (2%)
  starting transfers between devices  39.9 us (2%)
    reduce_scatter x1, waiting for transfers between devices, shards(): lax.psum_scatter(g_sdown, 'dp', scatter_dimension=1, tiled=True)  248 us
    reduce_scatter x1, waiting for transfers between devices, shards(): lax.psum_scatter(g_sup, 'dp', scatter_dimension=0, tiled=True)  248 us
    reduce_scatter x1, waiting for transfers between devices, shards(): lax.psum_scatter(g_query, 'dp', scatter_dimension=0, tiled=True)  211 us
    reduce_scatter x1, waiting for transfers between devices, shards(): lax.psum_scatter(g_out, 'dp', scatter_dimension=1, tiled=True)  180 us
    reduce_scatter x1, waiting for transfers between devices, shards(): lax.psum_scatter(g_latent, 'dp', scatter_dimension=0, tiled=True)  144 us
    unnamed x2, blocking collectives  129 us
    all_gather x1, blocking collectives, shards(): lax.all_gather(norm_gain, 'dp', axis=0, tiled=True)  111 us
    all_gather x1, waiting for transfers between devices, shards(): lax.all_gather(shared_down, 'dp', axis=1, tiled=True)  104 us
  transfers between devices with their start and end apart: 24, of which 17 were waited for; matrix products, arithmetic and copies ran while one was open for 12% of the time, Pallas kernels for 0%

commit v1 on v0

--- a/solution.py
+++ b/solution.py
@@ -1,6 +1,10 @@
+import functools
+
 import jax
 import jax.numpy as jnp
 from jax import lax
+from jax.experimental import pallas as pl
+from jax.experimental.pallas import tpu as pltpu
 from jax.sharding import PartitionSpec as P
 
 NOPE = 128
@@ -332,6 +336,740 @@
     )
 
 
+MESH = pl.DeviceIdType.MESH
+
+
+def place_of(grid):
+    index = lax.axis_index("dp")
+    place = []
+    for size in reversed(grid):
+        place.append(lax.rem(index, size))
+        index = index // size
+    return tuple(reversed(place)) + (lax.axis_index("tensor"),)
+
+
+def device_at(grid, place):
+    index = place[0]
+    for size, spot in zip(grid[1:], place[1:-1]):
+        index = index * size + spot
+    return (index, place[-1])
+
+
+def moved(place, dim, spot):
+    return tuple(spot if axis == dim else at for axis, at in enumerate(place))
+
+
+def greet(grid, place):
+    sizes = grid + (2,)
+    barrier = pltpu.get_barrier_semaphore()
+    for dim, size in enumerate(sizes):
+        for step in (-1, 1):
+            if size == 2:
+                if step == 1:
+                    pl.semaphore_signal(barrier, inc=1, device_id=device_at(grid, moved(place, dim, 1 - place[dim])), device_id_type=MESH)
+                continue
+            spot = place[dim] + step
+
+            @pl.when((spot >= 0) & (spot < size))
+            def _():
+                pl.semaphore_signal(barrier, inc=1, device_id=device_at(grid, moved(place, dim, spot)), device_id_type=MESH)
+
+    peers = 0
+    for dim, size in enumerate(sizes):
+        if size == 2:
+            peers += 1
+        else:
+            peers += jnp.minimum(place[dim], 1) + jnp.minimum(size - 1 - place[dim], 1)
+    pl.semaphore_wait(barrier, peers)
+
+
+def stage_plan(sizes, order, weight, first):
+    plan, now, held = [], 0.0, 1
+    for dim in order:
+        for step in range(sizes[dim] - 1):
+            cost = weight * held * (0.15 if dim == 3 else 1.0)
+            plan.append((now, dim, step))
+            now += cost
+        held *= sizes[dim]
+    plan.append((now, None, 0))
+    return plan
+
+
+def gather_body(grid, pieces, shared_flags, input_count, *refs):
+    sizes = grid + (2,)
+    inputs = refs[:input_count]
+    outputs = refs[input_count : 2 * input_count]
+    send_sem, recv_sem, own_sem = refs[2 * input_count :]
+    place = place_of(grid)
+
+    def window(number, piece, chosen):
+        which, start, rows, order = piece
+        spots = tuple(chosen.get(dim, place[dim]) for dim in range(4 if shared_flags[which] else 3))
+        return outputs[which].at[spots + (pl.ds(start, rows),)]
+
+    own = []
+    for number, piece in enumerate(pieces):
+        which, start, rows, order = piece
+        copy = pltpu.make_async_copy(inputs[which].at[pl.ds(start, rows)], window(number, piece, {}), own_sem.at[number])
+        copy.start()
+        own.append(copy)
+    greet(grid, place)
+
+    stages = []
+    for number, piece in enumerate(pieces):
+        which, start, rows, order = piece
+        weight = rows * inputs[which].shape[1]
+        for rank, (when, dim, step) in enumerate(stage_plan(sizes, order, weight, 0.0)):
+            stages.append((when, number, rank, dim, step))
+    stages.sort(key=lambda s: s[:3])
+    pending_recv = {number: [] for number in range(len(pieces))}
+    sends = []
+    slot_of = {}
+
+    def copies(number, rank, dim, step):
+        piece = pieces[number]
+        which, start, rows, order = piece
+        gathered = {}
+        for earlier in order[: order.index(dim)]:
+            gathered[earlier] = slice(None)
+        size = sizes[dim]
+        made = []
+        base = 2 * rank
+        if size == 2:
+            part = window(number, piece, gathered)
+            if not gathered:
+                source = inputs[which].at[pl.ds(start, rows)]
+            else:
+                source = part
+            copy = pltpu.make_async_remote_copy(
+                source, part, send_sem.at[number, base], recv_sem.at[number, base],
+                device_id=device_at(grid, moved(place, dim, 1 - place[dim])), device_id_type=MESH)
+            made.append((None, None, copy))
+            return made
+        for way, sign in enumerate((1, -1)):
+            spot = place[dim] + sign
+            block = place[dim] - sign * step
+            inside = (spot >= 0) & (spot < size) & (block >= 0) & (block < size)
+            back = place[dim] - sign
+            back_block = back - sign * step
+            arrives = (back >= 0) & (back < size) & (back_block >= 0) & (back_block < size)
+            chosen = dict(gathered)
+            chosen[dim] = jnp.clip(block, 0, size - 1)
+            part = window(number, piece, chosen)
+            if not gathered and step == 0:
+                source = inputs[which].at[pl.ds(start, rows)]
+            else:
+                source = part
+            copy = pltpu.make_async_remote_copy(
+                source, part, send_sem.at[number, base + way], recv_sem.at[number, base + way],
+                device_id=device_at(grid, moved(place, dim, jnp.clip(spot, 0, size - 1))), device_id_type=MESH)
+            made.append((inside, arrives, copy))
+        return made
+
+    for when, number, rank, dim, step in stages:
+        for condition, copy in pending_recv[number]:
+            if condition is None:
+                copy.wait_recv()
+            else:
+                pl.when(condition)(copy.wait_recv)
+        pending_recv[number] = []
+        if rank == 1:
+            own[number].wait()
+        if dim is None:
+            continue
+        for send_ok, recv_ok, copy in copies(number, rank, dim, step):
+            if send_ok is None:
+                copy.start()
+            else:
+                pl.when(send_ok)(copy.start)
+            sends.append((send_ok, copy))
+            pending_recv[number].append((recv_ok, copy))
+    for condition, copy in sends:
+        if condition is None:
+            copy.wait_send()
+        else:
+            pl.when(condition)(copy.wait_send)
+
+
+def gather(grid, arrays, shared_flags, pieces, collective_id):
+    out_shape = [
+        jax.ShapeDtypeStruct(grid + ((2,) if shared else ()) + array.shape, array.dtype)
+        for array, shared in zip(arrays, shared_flags)
+    ]
+    most = sum(size - 1 for size in grid) + 1
+    return pl.pallas_call(
+        functools.partial(gather_body, grid, pieces, shared_flags, len(arrays)),
+        out_shape=out_shape,
+        in_specs=[pl.BlockSpec(memory_space=pltpu.VMEM)] * len(arrays),
+        out_specs=[pl.BlockSpec(memory_space=pl.ANY)] * len(arrays),
+        scratch_shapes=[
+            pltpu.SemaphoreType.DMA((len(pieces), 2 * most)),
+            pltpu.SemaphoreType.DMA((len(pieces), 2 * most)),
+            pltpu.SemaphoreType.DMA((len(pieces),)),
+        ],
+        compiler_params=pltpu.CompilerParams(collective_id=collective_id, has_side_effects=True, vmem_limit_bytes=16 << 20),
+        name="gather_rows",
+    )(*arrays)
+
+
+def reduce_plan(sizes, order, weight):
+    plan, now, held = [], 0.0, 1
+    for dim in order:
+        held *= sizes[dim]
+    for dim in order:
+        held //= sizes[dim]
+        for step in range(sizes[dim] - 1):
+            plan.append((now, dim, step))
+            now += weight * held * (0.25 if dim == 3 else 1.0)
+    plan.append((now, None, 0))
+    return plan
+
+
+def landing_shapes(sizes, order, rows, width):
+    shapes = []
+    for rank, dim in enumerate(order):
+        left = tuple(sizes[d] for d in sorted(order[rank + 1 :]))
+        ways = 1 if sizes[dim] == 2 else 2
+        shapes.extend([left + (rows, width)] * (ways * (sizes[dim] - 1)))
+    return shapes
+
+
+def kept_index(place, later, dim, dims, kept, spots):
+    left = sorted(later)
+    return tuple(spots[left.index(d)] if d in later else (kept if d == dim else place[d]) for d in range(dims))
+
+
+def add_into(target, target_index, source, lead, rows):
+    chunk = 16
+    total = 1
+    for size in lead:
+        total *= size
+
+    def step(number, carry):
+        block, row = number // (rows // chunk), lax.rem(number, rows // chunk)
+        spots, rest = [], block
+        for size in reversed(lead):
+            spots.append(lax.rem(rest, size))
+            rest = rest // size
+        spots = tuple(reversed(spots))
+        span = pl.ds(pl.multiple_of(row * chunk, chunk), chunk)
+        here = target_index(spots) + (span,)
+        value = target[here].astype(jnp.float32) + source[spots + (span,)].astype(jnp.float32)
+        target[here] = value.astype(target.dtype)
+        return carry
+
+    lax.fori_loop(0, total * (rows // chunk), step, 0)
+
+
+def reduce_body(grid, pieces, shared_flags, input_count, *refs):
+    sizes = grid + (2,)
+    inputs = refs[:input_count]
+    outputs = refs[input_count : 2 * input_count]
+    scratch = list(refs[2 * input_count :])
+    held = [scratch.pop(0) for _ in pieces]
+    landings = []
+    for which, start, rows, order in pieces:
+        count = len(landing_shapes(sizes, order, rows, inputs[which].shape[-1]))
+        landings.append([scratch.pop(0) for _ in range(count)])
+    send_sem, recv_sem, own_sem = scratch
+    place = place_of(grid)
+
+    loads = []
+    for number, (which, start, rows, order) in enumerate(pieces):
+        dims = 4 if shared_flags[which] else 3
+        source = inputs[which].at[(slice(None),) * dims + (pl.ds(start, rows),)]
+        copy = pltpu.make_async_copy(source, held[number], own_sem.at[number])
+        copy.start()
+        loads.append(copy)
+    greet(grid, place)
+
+    stages = []
+    for number, (which, start, rows, order) in enumerate(pieces):
+        weight = rows * inputs[which].shape[-1]
+        slot = 0
+        for rank, (when, dim, step) in enumerate(reduce_plan(sizes, order, weight)):
+            stages.append((when, number, rank, dim, step))
+    stages.sort(key=lambda s: s[:3])
+    pending = {number: [] for number in range(len(pieces))}
+    slots = {number: 0 for number in range(len(pieces))}
+    sends = []
+
+    for when, number, rank, dim, step in stages:
+        which, start, rows, order = pieces[number]
+        width = inputs[which].shape[-1]
+        dims = 4 if shared_flags[which] else 3
+        if rank == 0:
+            loads[number].wait()
+        for arrives, copy, add in pending[number]:
+            if arrives is None:
+                copy.wait_recv()
+                add()
+            else:
+
+                @pl.when(arrives)
+                def _():
+                    copy.wait_recv()
+                    add()
+
+        pending[number] = []
+        if dim is None:
+            result = outputs[which]
+
+            def finish(chunk_number, carry):
+                span = pl.ds(pl.multiple_of(chunk_number * 16, 16), 16)
+                value = held[number][tuple(place[:dims]) + (span,)].astype(jnp.float32)
+                result[pl.ds(pl.multiple_of(start + chunk_number * 16, 16), 16)] = value
+                return carry
+
+            lax.fori_loop(0, rows // 16, finish, 0)
+            continue
+        later = order[order.index(dim) + 1 :]
+        lead = tuple(sizes[d] for d in sorted(later))
+        size = sizes[dim]
+
+        def whole(block):
+            return tuple(slice(None) if d in later else (block if d == dim else place[d]) for d in range(dims))
+
+        for sign in (1,) if size == 2 else (1, -1):
+            landing = landings[number][slots[number]]
+            sem = slots[number]
+            slots[number] += 1
+            if size == 2:
+                to, block, kept = 1 - place[dim], 1 - place[dim], place[dim]
+                goes = arrives = None
+            else:
+                to = place[dim] + sign
+                block = place[dim] + sign * (size - 1 - step)
+                back = place[dim] - sign
+                kept = place[dim] + sign * (size - 2 - step)
+                goes = (to >= 0) & (to < size) & (block >= 0) & (block < size)
+                arrives = (back >= 0) & (back < size) & (kept >= 0) & (kept < size)
+                to, block, kept = (jnp.clip(v, 0, size - 1) for v in (to, block, kept))
+            copy = pltpu.make_async_remote_copy(
+                held[number].at[whole(block)], landing, send_sem.at[number, sem], recv_sem.at[number, sem],
+                device_id=device_at(grid, moved(place, dim, to)), device_id_type=MESH)
+            if goes is None:
+                copy.start()
+            else:
+                pl.when(goes)(copy.start)
+            sends.append((goes, copy))
+
+            index = functools.partial(kept_index, place, later, dim, dims, kept)
+            add = functools.partial(add_into, held[number], index, landing, lead, rows)
+            pending[number].append((arrives, copy, add))
+    for condition, copy in sends:
+        if condition is None:
+            copy.wait_send()
+        else:
+            pl.when(condition)(copy.wait_send)
+
+
+def reduce(grid, arrays, shared_flags, pieces, collective_id):
+    sizes = grid + (2,)
+    out_shape = [
+        jax.ShapeDtypeStruct(array.shape[-2:], jnp.float32)
+        for array in arrays
+    ]
+    scratch, most = [], 1
+    for which, start, rows, order in pieces:
+        scratch.append(pltpu.VMEM(arrays[which].shape[:-2] + (rows, arrays[which].shape[-1]), arrays[which].dtype))
+    for which, start, rows, order in pieces:
+        shapes = landing_shapes(sizes, order, rows, arrays[which].shape[-1])
+        most = max(most, len(shapes) + 1)
+        scratch.extend(pltpu.VMEM(shape, arrays[which].dtype) for shape in shapes)
+    return pl.pallas_call(
+        functools.partial(reduce_body, grid, pieces, shared_flags, len(arrays)),
+        out_shape=out_shape,
+        in_specs=[pl.BlockSpec(memory_space=pl.ANY)] * len(arrays),
+        out_specs=[pl.BlockSpec(memory_space=pltpu.VMEM)] * len(arrays),
+        scratch_shapes=scratch + [
+            pltpu.SemaphoreType.DMA((len(pieces), most)),
+            pltpu.SemaphoreType.DMA((len(pieces), most)),
+            pltpu.SemaphoreType.DMA((len(pieces),)),
+        ],
+        compiler_params=pltpu.CompilerParams(collective_id=collective_id, has_side_effects=True, vmem_limit_bytes=60 << 20),
+        name="reduce_rows",
+    )(*arrays)
+
+
+def pair_body(grid, keep, count, *refs):
+    inputs, outputs = refs[:count], refs[count : 2 * count]
+    send_sem, recv_sem, own_sem = refs[2 * count :]
+    place = place_of(grid)
+    partner = device_at(grid, moved(place, 3, 1 - place[3]))
+    barrier = pltpu.get_barrier_semaphore()
+    pl.semaphore_signal(barrier, inc=1, device_id=partner, device_id_type=MESH)
+    own = []
+    for number in range(count if keep else 0):
+        copy = pltpu.make_async_copy(inputs[number], outputs[number].at[place[3]], own_sem.at[number])
+        copy.start()
+        own.append(copy)
+    pl.semaphore_wait(barrier, 1)
+    sent = []
+    for number in range(count):
+        target = outputs[number].at[place[3]] if keep else outputs[number]
+        copy = pltpu.make_async_remote_copy(
+            inputs[number], target, send_sem.at[number], recv_sem.at[number],
+            device_id=partner, device_id_type=MESH)
+        copy.start()
+        sent.append(copy)
+    for copy in own + sent:
+        copy.wait()
+
+
+def pair(grid, arrays, keep, collective_id):
+    count = len(arrays)
+    return pl.pallas_call(
+        functools.partial(pair_body, grid, keep, count),
+        out_shape=[jax.ShapeDtypeStruct(((2,) if keep else ()) + array.shape, array.dtype) for array in arrays],
+        in_specs=[pl.BlockSpec(memory_space=pltpu.VMEM if keep else pl.ANY)] * count,
+        out_specs=[pl.BlockSpec(memory_space=pl.ANY)] * count,
+        scratch_shapes=[pltpu.SemaphoreType.DMA((count,))] * 3,
+        compiler_params=pltpu.CompilerParams(
+            collective_id=collective_id, has_side_effects=True, vmem_limit_bytes=16 << 20),
+        name="pair_rows",
+    )(*arrays)
+
+
+Z, Y, X, C = 0, 1, 2, 3
+
+
+def cut(which, rows, orders, core_last=False, core_first=False):
+    chunks = rows // 16
+    total = sum(share for share, _ in orders)
+    pieces, start, used = [], 0, 0
+    for share, order in orders:
+        used += share
+        end = chunks * used // total * 16
+        if end > start:
+            full = ((C,) if core_first else ()) + order + ((C,) if core_last else ())
+            pieces.append((which, start, end - start, full))
+            start = end
+    return pieces
+
+
+GATHER_ORDERS = ((2, (Z, Y, X)), (2, (Z, X, Y)), (1, (Z, Y, X)), (1, (Z, X, Y)), (2, (Y, X, Z)))
+REDUCE_ORDERS = ((1, (X, Y, Z)), (1, (Y, X, Z))) * 3 + ((1, (Z, X, Y)),) * 2
+REDUCE_COARSE = ((2, (X, Y, Z)), (2, (Y, X, Z)), (1, (X, Y, Z)), (1, (Y, X, Z)), (2, (Z, X, Y)))
+
+
+def dense_shards(
+    grid,
+    hidden_in,
+    norm_gain,
+    w_query,
+    w_latent,
+    latent_gain,
+    w_up,
+    w_out,
+    ffn_gain,
+    shared_gate,
+    shared_up,
+    shared_down,
+    expert_gate,
+    expert_up,
+    expert_down,
+    gate_values,
+    expert_ids,
+    segment_ids,
+    cotangent,
+):
+    f32, bf16 = jnp.float32, jnp.bfloat16
+    length, width = hidden_in.shape
+    half = length // 2
+    topk_count = expert_ids.shape[1]
+    chips = lax.axis_size("dp")
+    head_count = w_query.shape[1] // (NOPE + ROPE)
+    kv_rank = latent_gain.shape[0] * chips
+    capacity = max(2, 2 * (length * topk_count * 7 // (12 * chips)))
+    core = lax.axis_index("tensor")
+    chip = lax.axis_index("dp")
+
+    def rows_of(array, which):
+        count = array.shape[0] // 2
+        return lax.dynamic_slice_in_dim(array, which * count, count, 0)
+
+    part_units = shared_gate.shape[1] // chips
+    model_rows = shared_gate.shape[0]
+    stacked = jnp.stack([shared_gate, shared_up, shared_down.T]).reshape(3, model_rows, chips, part_units)
+    resharded = lax.all_to_all(stacked.transpose(2, 0, 1, 3), "dp", split_axis=0, concat_axis=0, tiled=True)
+    s_gate, s_up, s_down_t = (resharded[:, i].reshape(width, part_units) for i in range(3))
+
+    gain_rows = norm_gain.shape[0]
+    latent_rows = latent_gain.shape[0]
+    gains = jnp.zeros((16, 3 * gain_rows), bf16)
+    gains = gains.at[0, :gain_rows].set(norm_gain).at[0, gain_rows : 2 * gain_rows].set(ffn_gain)
+    gains = gains.at[0, 2 * gain_rows : 2 * gain_rows + latent_rows].set(latent_gain)
+    named = expert_ids[:, :, None] == jnp.arange(chips, dtype=jnp.int32)[None, None, :]
+    gate_map = jnp.sum(jnp.where(named, gate_values[:, :, None], 0.0), axis=1).T
+    mine = [w_query, w_out.T, w_up, rows_of(w_latent, core), gains, gate_map]
+    shared = [False, False, False, True, False, False]
+    pieces = (
+        cut(0, mine[0].shape[0], GATHER_ORDERS)
+        + cut(1, mine[1].shape[0], GATHER_ORDERS)
+        + cut(2, mine[2].shape[0], ((1, (Z, Y, X)), (1, (Z, X, Y))))
+        + cut(3, mine[3].shape[0], ((1, (X, Y, Z)),), core_last=True)
+        + cut(4, mine[4].shape[0], ((1, (Z, Y, X)),))
+        + cut(5, mine[5].shape[0], ((1, (Z, X, Y)),))
+    )
+    got = gather(grid, mine, shared, pieces, 1)
+    full_query = got[0].reshape(width, -1)
+    full_out_t = got[1].reshape(width, -1)
+    full_up = got[2].reshape(kv_rank, -1)
+    full_latent = got[3].reshape(width, -1)
+    all_gains = got[4].reshape(chips, 16, -1)[:, 0].astype(f32)
+    gain_one = all_gains[:, :gain_rows].reshape(-1)
+    gain_two = all_gains[:, gain_rows : 2 * gain_rows].reshape(-1)
+    gain_latent = all_gains[:, 2 * gain_rows : 2 * gain_rows + latent_rows].reshape(-1)
+    gates = lax.dynamic_index_in_dim(got[5].reshape(chips, -1, length), chip, 1, keepdims=False)
+
+    cosine, sine = rope_tables(length)
+    scale = (NOPE + ROPE) ** (-0.5)
+    segment_row = segment_ids[0]
+    position = jnp.arange(length, dtype=jnp.int32)
+    allowed = (segment_row[:, None] == segment_row[None, :]) & (
+        position[None, :] <= position[:, None]
+    )
+    tokens_f = hidden_in.astype(f32)
+    normed_f, inverse_one = rms_forward(tokens_f, gain_one)
+    normed = normed_f.astype(bf16)
+    query_all = jnp.dot(normed, full_query, preferred_element_type=f32).reshape(
+        length, head_count, NOPE + ROPE
+    )
+    query_rope = rotate(query_all[..., NOPE:], cosine[:, None, :], sine[:, None, :])
+    queries = jnp.concatenate([query_all[..., :NOPE], query_rope], axis=-1).astype(bf16)
+    latent_all = jnp.dot(normed, full_latent, preferred_element_type=f32)
+    latent = latent_all[:, :kv_rank]
+    latent_normed, latent_inverse = rms_forward(latent, gain_latent)
+    latent_bf = latent_normed.astype(bf16)
+    key_rope = rotate(latent_all[:, kv_rank:], cosine, sine).astype(bf16)
+    expanded = jnp.dot(latent_bf, full_up, preferred_element_type=f32).astype(bf16)
+    expanded = expanded.reshape(length, head_count, NOPE + VDIM)
+    key_all = jnp.concatenate(
+        [expanded[..., :NOPE], jnp.broadcast_to(key_rope[:, None, :], (length, head_count, ROPE))],
+        axis=-1,
+    )
+    values = expanded[..., NOPE:]
+    scores = jnp.einsum("qhd,khd->hqk", queries, key_all, preferred_element_type=f32) * scale
+    raw_probs = jnp.where(allowed[None], jnp.exp(scores), 0.0)
+    totals = jnp.sum(raw_probs, axis=-1, keepdims=True)
+    log_total = jnp.log(totals)
+    attn_weights = (raw_probs / totals).astype(bf16)
+    context = jnp.einsum("hqk,khd->qhd", attn_weights, values, preferred_element_type=f32)
+    context = context.reshape(length, head_count * VDIM).astype(bf16)
+    attended_part = lax.dot_general(
+        context, full_out_t, (((1,), (1,)), ((), ())), preferred_element_type=f32
+    )
+    (other,) = pair(grid, [rows_of(attended_part, 1 - core)], False, 5)
+    residual = rows_of(tokens_f, core) + (rows_of(attended_part, core) + other)
+    ffn_f, inverse_two = rms_forward(residual, gain_two)
+    ffn_in = ffn_f.astype(bf16)
+
+    cot_half = rows_of(cotangent, core)
+    pieces = cut(0, half, GATHER_ORDERS, core_last=True) + cut(1, half, GATHER_ORDERS, core_last=True)
+    ffn_all, cot_all = gather(grid, [ffn_in, cot_half.astype(bf16)], [True, True], pieces, 2)
+    ffn_all = ffn_all.reshape(-1, width)
+    cot_all = cot_all.reshape(-1, width)
+
+    routed = gates > 0.0
+    triangle = (position[:, None] < position[None, :]).astype(bf16)
+    slot = jnp.dot(routed.astype(bf16), triangle, preferred_element_type=f32).astype(jnp.int32)
+    chosen = routed[:, None, :] & (slot[:, None, :] == jnp.arange(capacity, dtype=jnp.int32)[None, :, None])
+    pick = chosen.astype(bf16)
+    gate_slot = jnp.sum(jnp.where(chosen, gates[:, None, :], 0.0), axis=-1)[..., None]
+
+    def take(rows):
+        return jnp.einsum(
+            "sct,std->scd", pick, rows.reshape(chips, length, width), preferred_element_type=f32
+        )
+
+    def spread(rows):
+        return jnp.einsum(
+            "sct,scd->std", pick, rows.reshape(chips, capacity, width), preferred_element_type=f32
+        ).reshape(chips * length, width)
+
+    expert_rows = take(ffn_all).astype(bf16).reshape(-1, width)
+    grad_rows = (gate_slot * take(cot_all)).astype(bf16).reshape(-1, width)
+    gate_rows = gate_slot.reshape(-1, 1)
+    local_gate, local_up, local_down = expert_gate[0], expert_up[0], expert_down[0]
+    gate_projected = jnp.dot(expert_rows, local_gate, preferred_element_type=f32)
+    up_projected = jnp.dot(expert_rows, local_up, preferred_element_type=f32)
+    expert_hidden = (jax.nn.silu(gate_projected) * up_projected).astype(bf16)
+    expert_part = jnp.dot(expert_hidden, local_down, preferred_element_type=f32)
+    weighted = (gate_rows * expert_part).astype(bf16)
+    shared_g = jnp.dot(ffn_all, s_gate, preferred_element_type=f32)
+    shared_u = jnp.dot(ffn_all, s_up, preferred_element_type=f32)
+    shared_hidden = (jax.nn.silu(shared_g) * shared_u).astype(bf16)
+    shared_part = lax.dot_general(
+        shared_hidden, s_down_t, (((1,), (1,)), ((), ())), preferred_element_type=f32
+    )
+    forward_part = (shared_part + spread(weighted)).astype(bf16)
+    block_shape = grid + (2, half, width)
+    reduce_pieces = cut(0, half, REDUCE_ORDERS, core_first=True)
+    (ffn_total,) = reduce(grid, [forward_part.reshape(block_shape)], [True], reduce_pieces, 3)
+    output_half = (residual + ffn_total).astype(bf16)
+
+    hidden_gradient = lax.dot_general(
+        grad_rows, local_down, (((1,), (1,)), ((), ())), preferred_element_type=f32
+    )
+    gate_gradient = (hidden_gradient * up_projected * silu_slope(gate_projected)).astype(bf16)
+    up_gradient = (hidden_gradient * jax.nn.silu(gate_projected)).astype(bf16)
+    back_part = lax.dot_general(
+        gate_gradient, local_gate, (((1,), (1,)), ((), ())), preferred_element_type=f32
+    ) + lax.dot_general(up_gradient, local_up, (((1,), (1,)), ((), ())), preferred_element_type=f32)
+    shared_hg = jnp.dot(cot_all, s_down_t, preferred_element_type=f32)
+    grad_sgate = (shared_hg * shared_u * silu_slope(shared_g)).astype(bf16)
+    grad_sup = (shared_hg * jax.nn.silu(shared_g)).astype(bf16)
+    shared_back = lax.dot_general(
+        grad_sgate, s_gate, (((1,), (1,)), ((), ())), preferred_element_type=f32
+    ) + lax.dot_general(grad_sup, s_up, (((1,), (1,)), ((), ())), preferred_element_type=f32)
+    backward_part = (shared_back + spread(back_part.astype(bf16))).astype(bf16)
+    (grad_ffn,) = reduce(grid, [backward_part.reshape(block_shape)], [True], reduce_pieces, 3)
+
+    grad_expert_down = jnp.dot(expert_hidden.T, grad_rows, preferred_element_type=f32)
+    grad_expert_gate = jnp.dot(expert_rows.T, gate_gradient, preferred_element_type=f32)
+    gradient_expert_upward = jnp.dot(expert_rows.T, up_gradient, preferred_element_type=f32)
+    shared_grads = jnp.stack(
+        [
+            jnp.dot(ffn_all.T, grad_sgate, preferred_element_type=f32),
+            jnp.dot(ffn_all.T, grad_sup, preferred_element_type=f32),
+            jnp.dot(cot_all.T, shared_hidden, preferred_element_type=f32),
+        ]
+    ).astype(bf16)
+    returned = lax.all_to_all(
+        shared_grads.reshape(3, chips, model_rows, part_units).transpose(1, 0, 2, 3),
+        "dp",
+        split_axis=0,
+        concat_axis=0,
+        tiled=True,
+    )
+    returned = returned.transpose(1, 2, 0, 3).reshape(3, model_rows, -1).astype(f32)
+    s_sgate, s_sup, s_sdown = returned[0], returned[1], returned[2].T
+
+    grad_res_part, g_fgain = rms_backward(residual, inverse_two, gain_two, grad_ffn)
+    grad_residual = cot_half + grad_res_part
+    (grad_attn,) = pair(grid, [grad_residual.astype(bf16)], True, 6)
+    grad_attn = grad_attn.reshape(length, width)
+    g_out_t = jnp.dot(grad_attn.T, context, preferred_element_type=f32)
+    grad_context = (
+        jnp.dot(grad_attn, full_out_t, preferred_element_type=f32)
+        .astype(bf16)
+        .reshape(length, head_count, VDIM)
+    )
+    probs = jnp.where(allowed[None], jnp.exp(scores - log_total), 0.0)
+    weights_back = probs.astype(bf16)
+    grad_values = jnp.einsum("hqk,qhd->khd", weights_back, grad_context, preferred_element_type=f32)
+    grad_weights = jnp.einsum("qhd,khd->hqk", grad_context, values, preferred_element_type=f32)
+    row_delta = jnp.sum(probs * grad_weights, axis=-1, keepdims=True)
+    grad_scores = (probs * (grad_weights - row_delta) * scale).astype(bf16)
+    grad_queries = jnp.einsum("hqk,khd->qhd", grad_scores, key_all, preferred_element_type=f32)
+    grad_keys = jnp.einsum("hqk,qhd->khd", grad_scores, queries, preferred_element_type=f32)
+    grad_qrope = rotate(grad_queries[..., NOPE:], cosine[:, None, :], -sine[:, None, :])
+    grad_query_all = (
+        jnp.concatenate([grad_queries[..., :NOPE], grad_qrope], axis=-1)
+        .reshape(length, head_count * (NOPE + ROPE))
+        .astype(bf16)
+    )
+    grad_expanded = (
+        jnp.concatenate([grad_keys[..., :NOPE], grad_values], axis=-1)
+        .reshape(length, head_count * (NOPE + VDIM))
+        .astype(bf16)
+    )
+    g_up = jnp.dot(latent_bf.T, grad_expanded, preferred_element_type=f32)
+    g_query = jnp.dot(normed.T, grad_query_all, preferred_element_type=f32)
+    latent_part = lax.dot_general(
+        grad_expanded, full_up, (((1,), (1,)), ((), ())), preferred_element_type=f32
+    )
+    rope_part = rotate(jnp.sum(grad_keys[..., NOPE:], axis=1), cosine, -sine)
+    latent_part = jnp.concatenate([latent_part, rope_part], axis=-1)
+    input_part = lax.dot_general(
+        grad_query_all, full_query, (((1,), (1,)), ((), ())), preferred_element_type=f32
+    )
+    latent_other, input_other = pair(
+        grid, [rows_of(latent_part, 1 - core), rows_of(input_part, 1 - core)], False, 7
+    )
+    latent_sum = rows_of(latent_part, core) + latent_other
+    grad_latent, g_lgain = rms_backward(
+        rows_of(latent, core), rows_of(latent_inverse, core), gain_latent, latent_sum[:, :kv_rank]
+    )
+    grad_latent_all = jnp.concatenate([grad_latent, latent_sum[:, kv_rank:]], axis=-1).astype(bf16)
+    g_latent = jnp.dot(rows_of(normed, core).T, grad_latent_all, preferred_element_type=f32)
+    grad_normed = (rows_of(input_part, core) + input_other) + lax.dot_general(
+        grad_latent_all, full_latent, (((1,), (1,)), ((), ())), preferred_element_type=f32
+    )
+    grad_in_part, g_norm = rms_backward(
+        rows_of(tokens_f, core), rows_of(inverse_one, core), gain_one, grad_normed
+    )
+    grad_input_half = grad_residual + grad_in_part
+
+    g_gains = jnp.concatenate(
+        [
+            g_norm.reshape(chips, gain_rows),
+            g_fgain.reshape(chips, gain_rows),
+            jnp.pad(g_lgain.reshape(chips, latent_rows), ((0, 0), (0, gain_rows - latent_rows))),
+        ],
+        axis=1,
+    )
+    g_gains = jnp.pad(g_gains[:, None, :], ((0, 0), (0, 15), (0, 0)))
+    terms = [
+        g_query.astype(bf16).reshape(grid + (-1, g_query.shape[1])),
+        g_out_t.astype(bf16).reshape(grid + (-1, g_out_t.shape[1])),
+        g_up.astype(bf16).reshape(grid + (-1, g_up.shape[1])),
+        g_latent.astype(bf16).reshape(grid + (2, -1, g_latent.shape[1])),
+        g_gains.astype(bf16).reshape(grid + (16, -1)),
+    ]
+    pieces = (
+        cut(0, terms[0].shape[-2], REDUCE_COARSE)
+        + cut(1, terms[1].shape[-2], REDUCE_COARSE)
+        + cut(2, terms[2].shape[-2], ((1, (X, Y, Z)), (1, (Y, X, Z))))
+        + cut(3, terms[3].shape[-2], ((1, (Z, X, Y)),), core_first=True)
+        + cut(4, terms[4].shape[-2], ((1, (X, Y, Z)),))
+    )
+    s_query, s_out_t, s_up, latent_half, gain_sums = reduce(
+        grid, terms, [False, False, False, True, False], pieces, 4
+    )
+    output, grad_input, s_latent, gain_sums = pair(
+        grid, [output_half, grad_input_half, latent_half, gain_sums], True, 8
+    )
+    gain_sums = gain_sums[0, 0] + gain_sums[1, 0]
+    return (
+        output.reshape(length, width),
+        grad_input.reshape(length, width),
+        gain_sums[:gain_rows],
+        s_query,
+        s_latent.reshape(-1, s_latent.shape[-1]),
+        gain_sums[2 * gain_rows : 2 * gain_rows + latent_rows],
+        s_up,
+        s_out_t.T,
+        gain_sums[gain_rows : 2 * gain_rows],
+        s_sgate,
+        s_sup,
+        s_sdown,
+        grad_expert_gate[None],
+        gradient_expert_upward[None],
+        grad_expert_down[None],
+    )
+
+
+def chip_grid(mesh):
+    coords = [tuple(getattr(device, "coords", ())) for device in mesh.devices[:, 0]]
+    if any(len(spot) != 3 for spot in coords):
+        return None
+    low = [min(spot[axis] for spot in coords) for axis in range(3)]
+    sizes = [max(spot[axis] for spot in coords) - low[axis] + 1 for axis in range(3)]
+    steps = []
+    for axis in range(3):
+        steps.append(next((i for i, spot in enumerate(coords) if spot[axis] != low[axis]), 0))
+    order = sorted(range(3), key=lambda axis: -steps[axis])
+    grid = tuple(sizes[axis] for axis in order)
+    for index, spot in enumerate(coords):
+        for axis in reversed(order):
+            if index % sizes[axis] != spot[axis] - low[axis]:
+                return None
+            index //= sizes[axis]
+    return grid if min(grid) >= 2 else None
+
+
 def solution(mesh):
     in_specs = (
         P("dp", None),
@@ -370,4 +1108,13 @@
         P("dp", None, "tensor"),
         P("dp", "tensor", None),
     )
-    return jax.shard_map(shards, mesh=mesh, in_specs=in_specs, out_specs=out_specs, check_vma=False)
+    grid = chip_grid(mesh)
+
+    def step(*args):
+        dense = grid is not None and 4 * args[15].shape[1] >= mesh.shape["dp"]
+        body = functools.partial(dense_shards, grid) if dense else shards
+        return jax.shard_map(
+            body, mesh=mesh, in_specs=in_specs, out_specs=out_specs, check_vma=False
+        )(*args)
+
+    return step

time: 2580 us -> 1120 us (0.43)
  waiting for transfers between devices: 1700 us -> 0.01 us
  Pallas kernels: 0 us -> 622 us
  blocking collectives: 360 us -> 0 us
  matrix products: 222 us -> 304 us
  local copies, waits for them, and re-layouts: 165 us -> 131 us
  other arithmetic: 64 us -> 35.3 us
    reduce_scatter x9 -> x0, waiting for transfers between devices: 1250 us -> none  [the longest x1 248 us: shards(): lax.psum_scatter(g_sdown, 'dp', scatter_dimension=1, tiled=True)]
    pallas_call x0 -> x9, Pallas kernels: none -> 622 us  [the longest x3 336 us: reduce(): pl.pallas_call(functools.partial(reduce_body, grid, pieces, shared_flags,...]
    all_gather x9 -> x0, waiting for transfers between devices: 358 us -> none  [the longest x1 104 us: shards(): lax.all_gather(shared_down, 'dp', axis=1, tiled=True)]
    all_gather x2 -> x0, blocking collectives: 149 us -> none  [the longest x1 111 us: shards(): lax.all_gather(norm_gain, 'dp', axis=0, tiled=True)]
    unnamed x2 -> x0, blocking collectives: 129 us -> none
    dot_general x36 -> x41, matrix products: 222 us -> 304 us  [the longest x2 29.4 us: spread(): jnp.einsum('sct,scd->std', pick, rows.reshape(chips, capacity, width), pr...]
    all_to_all x1 -> x0, blocking collectives: 78.8 us -> none  [shards(): lax.all_to_all(portion, 'dp', split_axis=0, concat_axis=0, tiled=True)]
    all_to_all x3 -> x2, waiting for transfers between devices: 74.3 us -> 0.01 us  [the longest x1 0.01 us: dense_shards(): lax.all_to_all(stacked.transpose(2, 0, 1, 3), 'dp', split_axis=0, concat_...]
  transfers between devices with their start and end apart: 24 -> 2, of which waited for: 17 -> 0; matrix products, arithmetic and copies ran while one was open for 12% -> 25% of each run, Pallas kernels for 0% -> 41%
where the time goes in v1:
time: 1120 us; the launch traced here: 1110 us
  Pallas kernels  622 us (56%)
  matrix products  304 us (27%)
  local copies, waits for them, and re-layouts  131 us (12%)
  other arithmetic  35.3 us (3%)
  starting transfers between devices  14.4 us (1%)
    pallas_call x3, Pallas kernels, reduce(): pl.pallas_call(functools.partial(reduce_body, grid, pieces, shared_flags,...  336 us
    pallas_call x2, Pallas kernels, gather(): pl.pallas_call(functools.partial(gather_body, grid, pieces, shared_flags,...  274 us
    unnamed x237, local copies, waits for them, and re-layouts  48.8 us
    dot_general x2, matrix products, spread(): jnp.einsum('sct,scd->std', pick, rows.reshape(chips, capacity, width), pr...  29.4 us
    dot_general x1, matrix products, dense_shards(): lax.dot_general(grad_sup, s_up, (((1,), (1,)), ((), ())), preferred_eleme...  28.4 us
  transfers between devices with their start and end apart: 2, of which 0 were waited for; matrix products, arithmetic and copies ran while one was open for 25% of the time, Pallas kernels for 41%

profile of v1, /device:TPU:0, one launch (start us, length us, event | category | flops | bytes accessed | tf_op | source)
XLA Modules:
  0.0 1109.6 jit_solution(14543278501063652628)
XLA Ops:
  2.0 1.9 copy.188
  6.2 8.4 all-to-all-start
  16.7 2.9 convert_element_type.153
  21.5 2.0 broadcast_select_fusion.1
  25.0 2.0 broadcast_select_fusion
  33.9 121.6 %gather_rows.2 = (bf16[4,2,2,128,1536]{4,3,2,1,0:T(8,128)(2,1)S(1)}, bf16[4,2,2,128,1024]{4,3,2,1,0:T(8,128)(2,1)S(1)}, bf16[4,2,2,32,2048]{4,3,2,1,0:T(8,128)(2...) custom-call(bf16[128,1536]{1,0:T(8,128)(2,1)S(1)} %copy-done.13, ...), custom_call_target="tpu_custom_call" | custom-call | tf_op jit(solution)/shard_map/gather_rows/pallas_call | solution.py:500
  155.6 2.7 copy-done.4
  161.8 2.0 copy-done.19
  170.5 3.1 fusion.118
  181.4 3.5 convolution_convert_fusion.5
  184.9 2.3 copy.218
  189.1 8.6 copy.178
  197.7 5.0 fusion.41
  205.9 2.1 fusion.30
  212.6 2.7 pair_rows.4
  216.5 152.6 %gather_rows.3 = (bf16[4,2,2,2,128,2048]{5,4,3,2,1,0:T(8,128)(2,1)S(1)}, bf16[4,2,2,2,128,2048]{5,4,3,2,1,0:T(8,128)(2,1)S(1)}) custom-call(bf16[128,2048]{1,0:T(8,128)(2,1)S(1)} %multiply_convert_fusion.10.refs_0_, bf16[128,2048]{1,0:T(8,128)(2,1)S(1)} %dynamic-slice_convert_fusion.refs_1_), custom_call_target="tpu_custom_call" | custom-call | tf_op jit(solution)/shard_map/gather_rows/pallas_call | solution.py:500
  369.0 5.9 copy-done.2
  374.9 5.9 copy-done.3
  380.8 13.7 %multiply_convert_fusion = bf16[16,112,2048]{2,1,0:T(8,128)(2,1)} fusion(f32[16,112]{1,0:T(8,128)S(1)} %select_reduce_fusion, bf16[16,256,2048]{2,1,0:T(8,128)(2,1)} %bitcast.240, s32[16,256]{1,0:T(8,128)S(1)} %convolution_convert_fusion.11, pred[16,256]{1,0:T(8,128)(4,1)S(1)} %compare_bitcast_fusion), kind=kOutput, calls=%fused_computation.6 | convolution fusion | flops 1887305728 | bytes 24144896 | tf_op jit(solution)/shard_map/sct,std->scd/dot_general | solution.py:882
  394.4 8.1 convolution_convert_fusion.1
  402.6 9.9 fusion.8
  412.5 7.1 fusion.12
  419.6 12.1 %multiply_convert_fusion.2 = (bf16[1792,704]{0,1:T(8,128)(2,1)}, bf16[1792,704]{0,1:T(8,128)(2,1)}, bf16[1792,704]{0,1:T(8,128)(2,1)}) fusion(f32[1792,704]{0,1:T(8,128)} %fusion.12, f32[1792,704]{0,1:T(8,128)} %fusion.8, bf16[1792,2048]{1,0:T(8,128)(2,1)S(1)} %bitcast.279, bf16[1,704,2048]{2,1,0:T(8,128)(2,1)S(1)} %copy-done), kind=kOutput, calls=%fused_computation.9 | convolution fusion | flops 5186306048 | bytes 27885568 | tf_op jit(solution)/shard_map/dot_general | solution.py:912
  431.7 9.1 convolution_bitcast_fusion.2
  440.8 7.2 convolution_bitcast_fusion
  448.0 6.2 multiply_convert_fusion.1
  454.2 9.4 fusion.10
  463.6 11.1 %add_convert_fusion = bf16[1792,2048]{1,0:T(8,128)(2,1)} fusion(f32[1792,2048]{1,0:T(8,128)} %fusion.10, bf16[1792,704]{0,1:T(8,128)(2,1)S(1)} %copy-done.96, bf16[1,2048,704]{1,2,0:T(8,128)(2,1)S(1)} %copy-done.92), kind=kOutput, calls=%fused_computation.5 | convolution fusion | flops 5174722560 | bytes 27426816 | tf_op jit(solution)/shard_map/dot_general | solution.py:919
  474.8 16.3 %fusion.18 = f32[16,256,2048]{2,1,0:T(8,128)} fusion(bf16[16,112,2048]{2,1,0:T(8,128)(2,1)} %bitcast.276, s32[16,256]{1,0:T(8,128)S(1)} %convolution_convert_fusion.11, pred[16,256]{1,0:T(8,128)(4,1)S(1)} %compare_bitcast_fusion), kind=kOutput, calls=%fused_computation.46 | convolution fusion | flops 1879965696 | bytes 40914944 | tf_op jit(solution)/shard_map/sct,scd->std/dot_general | solution.py:887
  491.1 13.2 %fusion.21 = f32[16,256,2048]{2,1,0:T(8,128)} fusion(bf16[16,112,2048]{2,1,0:T(8,128)(2,1)S(1)} %bitcast.275, s32[16,256]{1,0:T(8,128)S(1)} %convolution_convert_fusion.11, pred[16,256]{1,0:T(8,128)(4,1)S(1)} %compare_bitcast_fusion), kind=kOutput, calls=%fused_computation.47 | convolution fusion | flops 1879965696 | bytes 40914944 | tf_op jit(solution)/shard_map/sct,scd->std/dot_general | solution.py:887
  505.6 21.0 %copy.206 = bf16[2048,4096]{1,0:T(8,128)(2,1)} copy(bf16[2048,4096]{0,1:T(8,128)(2,1)} %bitcast.241) | data formatting | bytes 33554432 | tf_op jit(solution)/shard_map/dot_general | solution.py:936
  526.6 21.6 %copy.205 = bf16[2048,4096]{1,0:T(8,128)(2,1)} copy(bf16[2048,4096]{0,1:T(8,128)(2,1)} %bitcast.237) | data formatting | bytes 33554432 | tf_op jit(solution)/shard_map/dot_general | solution.py:934
  548.2 10.6 convolution_bitcast_fusion.1
  560.3 12.2 %fusion.68 = f32[4096,88]{0,1:T(8,128)} fusion(bf16[4096,2048]{1,0:T(8,128)(2,1)} %bitcast.238, bf16[11,8,16,128]{3,2,1,0:T(8,128)(2,1)S(1)} %bitcast.291), kind=kOutput, calls=%fused_computation.116 | convolution fusion | flops 1476395008 | bytes 18579456 | tf_op jit(solution)/shard_map/dot_general | solution.py:901
  572.6 12.3 %fusion.65 = f32[4096,88]{0,1:T(8,128)} fusion(bf16[4096,2048]{1,0:T(8,128)(2,1)} %bitcast.239, bf16[11,8,16,128]{3,2,1,0:T(8,128)(2,1)S(1)} %bitcast.289), kind=kOutput, calls=%fused_computation.113 | convolution fusion | flops 1476395008 | bytes 18579456 | tf_op jit(solution)/shard_map/dot_general | solution.py:900
  584.9 7.6 multiply_convert_fusion.7
  592.5 13.4 %fusion.63 = f32[4096,2048]{1,0:T(8,128)} fusion(bf16[4096,88]{0,1:T(8,128)(2,1)S(1)} %get-tuple-element.182, bf16[11,8,16,128]{3,2,1,0:T(8,128)(2,1)S(1)} %bitcast.290), kind=kOutput, calls=%fused_computation.111 | convolution fusion | flops 1476395008 | bytes 34635776 | tf_op jit(solution)/shard_map/dot_general | solution.py:923
  605.9 6.0 fusion.38
  611.9 6.0 fusion.39
  617.9 18.9 %fusion.2 = bf16[4096,2048]{1,0:T(8,128)(2,1)} fusion(f32[16,256,2048]{2,1,0:T(8,128)} %fusion.21, bf16[4096,88]{0,1:T(8,128)(2,1)S(1)} %get-tuple-element.183, bf16[11,8,16,128]{3,2,1,0:T(8,128)(2,1)S(1)} %bitcast.302), kind=kOutput, calls=%fused_computation.4 | convolution fusion | flops 1493172224 | bytes 51412992 | tf_op jit(solution)/shard_map/dot_general | solution.py:903
  636.8 83.4 %reduce_rows.3 = f32[128,2048]{1,0:T(8,128)} custom-call(bf16[4,2,2,2,128,2048]{5,4,3,2,1,0:T(8,128)(2,1)} %bitcast.267), custom_call_target="tpu_custom_call" | custom-call | tf_op jit(solution)/shard_map/reduce_rows/pallas_call | solution.py:680
  720.2 28.4 %fusion.1 = bf16[4096,2048]{1,0:T(8,128)(2,1)} fusion(f32[16,256,2048]{2,1,0:T(8,128)} %fusion.18, f32[4096,2048]{1,0:T(8,128)} %fusion.63, bf16[4096,88]{0,1:T(8,128)(2,1)S(1)} %get-tuple-element.181, bf16[11,8,16,128]{3,2,1,0:T(8,128)(2,1)S(1)} %bitcast.292), kind=kOutput, calls=%fused_computation.2 | convolution fusion | flops 1501560832 | bytes 84967424 | tf_op jit(solution)/shard_map/dot_general | solution.py:925
  748.6 82.4 %reduce_rows.4 = f32[128,2048]{1,0:T(8,128)} custom-call(bf16[4,2,2,2,128,2048]{5,4,3,2,1,0:T(8,128)(2,1)} %bitcast.266), custom_call_target="tpu_custom_call" | custom-call | tf_op jit(solution)/shard_map/reduce_rows/pallas_call | solution.py:680
  832.9 2.8 fusion.111
  835.7 1.9 pair_rows.5
  837.6 2.1 convolution_convert_fusion.7
  844.3 6.1 fusion.31
  850.4 5.1 fusion.34
  858.1 4.4 convolution_convert_fusion.2
  862.5 8.9 fusion.40
  872.6 6.1 all-to-all-start.1
  885.7 4.6 fusion.120
  890.5 3.2 pair_rows.6
  897.0 3.2 convolution_convert_fusion.3
  900.3 3.7 multiply_reduce_fusion.3
  904.7 4.5 copy.203
  909.2 2.2 convolution_convert_fusion.4
  911.4 4.5 convolution_convert_fusion
  915.9 170.4 %reduce_rows.5 = (f32[128,1536]{1,0:T(8,128)}, f32[128,1024]{1,0:T(8,128)}, f32[32,2048]{1,0:T(8,128)}, f32[64,576]{1,0:T(8,128)}, f32[16,384]{1,0:T(8,128)}) custom-call(bf16[4,2,2,128,1536]{4,3,2,1,0:T(8,128)(2,1)} %bitcast.269, bf16[4,2,2,128,1024]{4,3,2,1,0:T(8,128)(2,1)} %bitcast.270, bf16[4,2,2,32,2048]{4,3,2,1,0:T(8,128)(2,1)} %bitcast.282, ...), custom_call_target="tpu_custom_call" | custom-call | tf_op jit(solution)/shard_map/reduce_rows/pallas_call | solution.py:680
  1086.3 2.0 copy.209
  1088.3 1.9 subtract_add_fusion.refs_1_
  1090.3 3.8 pair_rows.7
  1102.1 2.5 copy.269
  1104.6 3.2 copy.270
  (319 shorter events, 78.1 us)
Async XLA Ops:
  0.6 419.0 %copy-start = (bf16[1,704,2048]{2,1,0:T(8,128)(2,1)S(1)}, bf16[1,704,2048]{2,1,0:T(8,128)(2,1)}, u32[]{:S(2)}) copy-start(bf16[1,704,2048]{2,1,0:T(8,128)(2,1)} %param.37) | copy-start | bytes 8650756
  6.2 552.6 %all-to-all-start = ((bf16[16,3,128,88]{2,3,1,0:T(8,128)(2,1)}), bf16[16,3,128,88]{2,3,1,0:T(8,128)(2,1)}, u32[]{:S(2)}, u32[]{:S(2)}) async-start(bf16[16,3,128,88]{2,3,1,0:T(8,128)(2,1)} %copy.189), calls=%async_computation | async-start | bytes 2162688 | tf_op jit(solution)/shard_map/all_to_all | solution.py:795
  14.6 6.2 copy-start.89
  14.6 6.2 copy-start.90
  14.6 6.8 copy-start.82
  14.6 6.8 copy-start.87
  14.7 10.3 copy-start.88
  16.7 15.4 %copy-start.13 = (bf16[128,1536]{1,0:T(8,128)(2,1)S(1)}, bf16[128,1536]{1,0:T(8,128)(2,1)}, u32[]{:S(2)}) copy-start(bf16[128,1536]{1,0:T(8,128)(2,1)} %refs_0_.1) | copy-start | bytes 1179652
  163.8 9.9 copy-start.58
  163.8 52.5 %copy-start.60 = (f32[2048]{0:T(1024)}, f32[2048]{0:T(1024)S(1)}, u32[]{:S(2)}) copy-start(f32[2048]{0:T(1024)S(1)} %get-tuple-element.203) | copy-start | bytes 24580
  168.5 13.0 %copy-start.70 = (f32[512]{0:T(512)}, f32[512]{0:T(512)S(1)}, u32[]{:S(2)}) copy-start(f32[512]{0:T(512)S(1)} %mul.506) | copy-start | bytes 6148
  170.5 4.6 copy-start.83
  177.4 27.2 %copy-start.53 = (f32[256,32]{0,1:T(8,128)}, f32[256,32]{0,1:T(8,128)S(1)}, u32[]{:S(2)}) copy-start(f32[256,32]{0,1:T(8,128)S(1)} %copy.180) | copy-start | bytes 98308
  181.4 5.8 copy-start.72
  197.7 7.0 copy-start.67
  197.7 8.1 copy-start.62
  215.7 178.7 %copy-start.22 = (f32[128,2048]{1,0:T(8,128)}, f32[128,2048]{1,0:T(8,128)S(1)}, u32[]{:S(2)}) copy-start(f32[128,2048]{1,0:T(8,128)S(1)} %get-tuple-element.177) | copy-start | bytes 3145732
  216.3 178.1 %copy-start.78 = (f32[128]{0:T(128)}, f32[128]{0:T(128)S(1)}, u32[]{:S(2)}) copy-start(f32[128]{0:T(128)S(1)} %get-tuple-element.213) | copy-start | bytes 1540
  369.0 5.9 copy-start.2
  374.9 5.9 copy-start.3
  402.6 38.2 %copy-start.24 = (bf16[16,112,2048]{2,1,0:T(8,128)(2,1)}, bf16[16,112,2048]{2,1,0:T(8,128)(2,1)S(1)}, u32[]{:S(2)}) copy-start(bf16[16,112,2048]{2,1,0:T(8,128)(2,1)S(1)} %convolution_convert_fusion.1) | copy-start | bytes 22020100
  402.6 9.9 copy-start.91
  402.6 17.0 %slice-start.8 = ((s8[7340032]{0:T(1024)(128)(4,1)}), s8[4194304]{0:T(1024)(128)(4,1)S(1)}, s32[]{:S(2)}) async-start(s8[7340032]{0:T(1024)(128)(4,1)} %bitcast.277), calls=%async_computation.10 | async-start | bytes 8388608
  412.5 7.1 slice-start.9
  431.7 9.1 copy-start.95
  440.8 7.2 copy-start.99
  448.0 6.2 copy-start.97
  454.2 9.4 copy-start.92
  454.2 9.4 copy-start.96
  491.0 13.2 %copy-start.73 = (f32[256]{0:T(256)S(1)}, f32[256]{0:T(256)}, u32[]{:S(2)}) copy-start(f32[256]{0:T(256)} %copy-done.72) | copy-start | bytes 3076
  491.1 13.8 %copy-start.76 = (f32[8,256]{1,0:T(8,128)S(1)}, f32[8,256]{1,0:T(8,128)}, u32[]{:S(2)}) copy-start(f32[8,256]{1,0:T(8,128)} %copy-done.75) | copy-start | bytes 24580
  491.1 13.8 %copy-start.51 = (f32[256,32]{1,0:T(8,128)S(1)}, f32[256,32]{1,0:T(8,128)}, u32[]{:S(2)}) copy-start(f32[256,32]{1,0:T(8,128)} %get-tuple-element.207) | copy-start | bytes 98308
  526.6 21.6 %copy-start.98 = (bf16[1792,704]{0,1:T(8,128)(2,1)S(1)}, bf16[1792,704]{0,1:T(8,128)(2,1)}, u32[]{:S(2)}) copy-start(bf16[1792,704]{0,1:T(8,128)(2,1)} %get-tuple-element.179) | copy-start | bytes 7569412
  560.3 24.6 %slice-start = ((s8[16777216]{0:T(1024)(128)(4,1)}), s8[4194304]{0:T(1024)(128)(4,1)S(1)}, s32[]{:S(2)}) async-start(s8[16777216]{0:T(1024)(128)(4,1)} %bitcast.242), calls=%async_computation.2 | async-start | bytes 8388608
  560.3 24.5 %slice-start.1 = ((s8[16777216]{0:T(1024)(128)(4,1)}), s8[4194304]{0:T(1024)(128)(4,1)S(1)}, s32[]{:S(2)}) async-start(s8[16777216]{0:T(1024)(128)(4,1)} %bitcast.242), calls=%async_computation.3 | async-start | bytes 8388608
  572.6 12.3 %slice-start.2 = ((s8[16777216]{0:T(1024)(128)(4,1)}), s8[4194304]{0:T(1024)(128)(4,1)S(1)}, s32[]{:S(2)}) async-start(s8[16777216]{0:T(1024)(128)(4,1)} %bitcast.242), calls=%async_computation.4 | async-start | bytes 8388608
  572.6 12.3 %slice-start.3 = ((s8[16777216]{0:T(1024)(128)(4,1)}), s8[4194304]{0:T(1024)(128)(4,1)S(1)}, s32[]{:S(2)}) async-start(s8[16777216]{0:T(1024)(128)(4,1)} %bitcast.242), calls=%async_computation.5 | async-start | bytes 8388608
  584.9 21.0 %slice-start.4 = ((s8[16777216]{0:T(1024)(128)(4,1)}), s8[4194304]{0:T(1024)(128)(4,1)S(1)}, s32[]{:S(2)}) async-start(s8[16777216]{0:T(1024)(128)(4,1)} %bitcast.262), calls=%async_computation.6 | async-start | bytes 8388608
  584.9 21.0 %slice-start.5 = ((s8[16777216]{0:T(1024)(128)(4,1)}), s8[4194304]{0:T(1024)(128)(4,1)S(1)}, s32[]{:S(2)}) async-start(s8[16777216]{0:T(1024)(128)(4,1)} %bitcast.262), calls=%async_computation.7 | async-start | bytes 8388608
  592.5 25.4 %copy-start.37 = (bf16[4096,88]{0,1:T(8,128)(2,1)}, bf16[4096,88]{0,1:T(8,128)(2,1)S(1)}, u32[]{:S(2)}) copy-start(bf16[4096,88]{0,1:T(8,128)(2,1)S(1)} %get-tuple-element.183) | copy-start | bytes 2162692
  592.5 13.4 %slice-start.6 = ((s8[16777216]{0:T(1024)(128)(4,1)}), s8[4194304]{0:T(1024)(128)(4,1)S(1)}, s32[]{:S(2)}) async-start(s8[16777216]{0:T(1024)(128)(4,1)} %bitcast.262), calls=%async_computation.8 | async-start | bytes 8388608
  592.5 13.4 %slice-start.7 = ((s8[16777216]{0:T(1024)(128)(4,1)}), s8[4194304]{0:T(1024)(128)(4,1)S(1)}, s32[]{:S(2)}) async-start(s8[16777216]{0:T(1024)(128)(4,1)} %bitcast.262), calls=%async_computation.9 | async-start | bytes 8388608
  748.6 82.5 %copy-start.23 = (f32[128,2048]{1,0:T(8,128)S(1)}, f32[128,2048]{1,0:T(8,128)}, u32[]{:S(2)}) copy-start(f32[128,2048]{1,0:T(8,128)} %copy-done.22) | copy-start | bytes 3145732
  748.6 82.5 %copy-start.61 = (f32[2048]{0:T(1024)S(1)}, f32[2048]{0:T(1024)}, u32[]{:S(2)}) copy-start(f32[2048]{0:T(1024)} %copy-done.60) | copy-start | bytes 24580
  748.6 82.5 %copy-start.79 = (f32[128]{0:T(128)S(1)}, f32[128]{0:T(128)}, u32[]{:S(2)}) copy-start(f32[128]{0:T(128)} %copy-done.78) | copy-start | bytes 1540
  748.6 84.2 %copy-start.86 = (f32[128]{0:T(128)S(1)}, f32[128]{0:T(128)}, u32[]{:S(2)}) copy-start(f32[128]{0:T(128)} %get-tuple-element.212) | copy-start | bytes 1540
  832.9 4.7 copy-start.21
  844.3 6.1 copy-start.64
  862.5 8.9 copy-start.44
  862.5 8.9 copy-start.45
  872.6 7.2 copy-start.8
  872.6 224.8 %all-to-all-start.1 = ((bf16[16,3,128,88]{2,3,1,0:T(8,128)(2,1)}), bf16[16,3,128,88]{2,3,1,0:T(8,128)(2,1)}, u32[]{:S(2)}, u32[]{:S(2)}) async-start(bf16[16,3,128,88]{2,3,1,0:T(8,128)(2,1)} %copy.207), calls=%async_computation.1 | async-start | bytes 2162688 | tf_op jit(solution)/shard_map/all_to_all | solution.py:939
  890.4 5.2 copy-start.42
  890.4 5.2 copy-start.71
  890.4 5.2 copy-start.77
  890.4 5.4 copy-start.81
  894.8 5.5 copy-start.6
  894.8 5.5 copy-start.59
  894.8 5.5 copy-start.80
  895.8 4.5 copy-start.12
  904.7 4.5 copy-start.74
  915.9 172.4 %copy-start.36 = (f32[128,2048]{1,0:T(8,128)S(1)}, f32[128,2048]{1,0:T(8,128)}, u32[]{:S(2)}) copy-start(f32[128,2048]{1,0:T(8,128)} %get-tuple-element.175) | copy-start | bytes 3145732
  915.9 172.5 %copy-start.85 = (f32[128]{0:T(128)S(1)}, f32[128]{0:T(128)}, u32[]{:S(2)}) copy-start(f32[128]{0:T(128)} %get-tuple-element.170) | copy-start | bytes 1540
  1102.1 7.3 copy-start.1
  (48 other events, 110.9 us)

commit v2 on v1

--- a/solution.py
+++ b/solution.py
@@ -750,7 +750,41 @@
 
 GATHER_ORDERS = ((2, (Z, Y, X)), (2, (Z, X, Y)), (1, (Z, Y, X)), (1, (Z, X, Y)), (2, (Y, X, Z)))
 REDUCE_ORDERS = ((1, (X, Y, Z)), (1, (Y, X, Z))) * 3 + ((1, (Z, X, Y)),) * 2
-REDUCE_COARSE = ((2, (X, Y, Z)), (2, (Y, X, Z)), (1, (X, Y, Z)), (1, (Y, X, Z)), (2, (Z, X, Y)))
+
+
+def spread_body(pick_ref, rows_ref, units_ref, weight_ref, out_ref):
+    routed = lax.dot_general(
+        pick_ref[0], rows_ref[0], (((0,), (0,)), ((), ())), preferred_element_type=jnp.float32
+    )
+    shared = lax.dot_general(
+        units_ref[...], weight_ref[...], (((1,), (1,)), ((), ())), preferred_element_type=jnp.float32
+    )
+    out_ref[...] = (routed + shared).astype(out_ref.dtype)
+
+
+def spread_rows(pick, rows, units, weight):
+    count, capacity, length = pick.shape
+    width = rows.shape[-1]
+    lanes = units.shape[-1]
+    return pl.pallas_call(
+        spread_body,
+        grid=(count,),
+        out_shape=jax.ShapeDtypeStruct((count * length, width), rows.dtype),
+        in_specs=[
+            pl.BlockSpec((1, capacity, length), lambda s: (s, 0, 0)),
+            pl.BlockSpec((1, capacity, width), lambda s: (s, 0, 0)),
+            pl.BlockSpec((length, lanes), lambda s: (s, 0)),
+            pl.BlockSpec((width, lanes), lambda s: (0, 0)),
+        ],
+        out_specs=pl.BlockSpec((length, width), lambda s: (s, 0)),
+        compiler_params=pltpu.CompilerParams(vmem_limit_bytes=32 << 20),
+        cost_estimate=pl.CostEstimate(
+            flops=2 * count * length * width * (capacity + lanes),
+            bytes_accessed=2 * count * (length + capacity) * width,
+            transcendentals=0,
+        ),
+        name="spread_rows",
+    )(pick, rows, units, weight)
 
 
 def dense_shards(
@@ -791,17 +825,25 @@
 
     part_units = shared_gate.shape[1] // chips
     model_rows = shared_gate.shape[0]
-    stacked = jnp.stack([shared_gate, shared_up, shared_down.T]).reshape(3, model_rows, chips, part_units)
-    resharded = lax.all_to_all(stacked.transpose(2, 0, 1, 3), "dp", split_axis=0, concat_axis=0, tiled=True)
-    s_gate, s_up, s_down_t = (resharded[:, i].reshape(width, part_units) for i in range(3))
-
+    lanes = -(-part_units // 128) * 128
+
+    def sliced(weight):
+        slices = weight.reshape(model_rows, chips, part_units).transpose(1, 0, 2)
+        return jnp.pad(slices, ((0, 0), (0, 0), (0, lanes - part_units)))
+
+    stacked = jnp.concatenate([sliced(shared_gate), sliced(shared_up), sliced(shared_down.T)], axis=2)
+    resharded = lax.all_to_all(stacked, "dp", split_axis=0, concat_axis=0, tiled=True)
+    resharded = resharded.reshape(width, 3 * lanes)
+    s_gate_up, s_down_t = resharded[:, : 2 * lanes], resharded[:, 2 * lanes :]
     gain_rows = norm_gain.shape[0]
     latent_rows = latent_gain.shape[0]
-    gains = jnp.zeros((16, 3 * gain_rows), bf16)
-    gains = gains.at[0, :gain_rows].set(norm_gain).at[0, gain_rows : 2 * gain_rows].set(ffn_gain)
-    gains = gains.at[0, 2 * gain_rows : 2 * gain_rows + latent_rows].set(latent_gain)
-    named = expert_ids[:, :, None] == jnp.arange(chips, dtype=jnp.int32)[None, None, :]
-    gate_map = jnp.sum(jnp.where(named, gate_values[:, :, None], 0.0), axis=1).T
+    gains = jnp.concatenate([norm_gain, ffn_gain, latent_gain])
+    gains = jnp.pad(gains[None], ((0, 15), (0, gain_rows - latent_rows)))
+    ids_t, gates_t = expert_ids.T, gate_values.T
+    numbers = jnp.arange(chips, dtype=jnp.int32)[:, None]
+    gate_map = jnp.zeros((chips, length), f32)
+    for k in range(topk_count):
+        gate_map += jnp.where(ids_t[k][None, :] == numbers, gates_t[k][None, :], 0.0)
     mine = [w_query, w_out.T, w_up, rows_of(w_latent, core), gains, gate_map]
     shared = [False, False, False, True, False, False]
     pieces = (
@@ -823,6 +865,14 @@
     gain_latent = all_gains[:, 2 * gain_rows : 2 * gain_rows + latent_rows].reshape(-1)
     gates = lax.dynamic_index_in_dim(got[5].reshape(chips, -1, length), chip, 1, keepdims=False)
 
+    def all_rows(part, after):
+        part, after = lax.optimization_barrier((part, after))
+        return lax.all_gather(part, ("dp", "tensor"), axis=0, tiled=True), after
+
+    cot_half = rows_of(cotangent, core)
+    cot_bf = cot_half.astype(bf16)
+    cot_left, gain_two = all_rows(cot_bf[:, : width // 2], gain_two)
+
     cosine, sine = rope_tables(length)
     scale = (NOPE + ROPE) ** (-0.5)
     segment_row = segment_ids[0]
@@ -833,9 +883,8 @@
     tokens_f = hidden_in.astype(f32)
     normed_f, inverse_one = rms_forward(tokens_f, gain_one)
     normed = normed_f.astype(bf16)
-    query_all = jnp.dot(normed, full_query, preferred_element_type=f32).reshape(
-        length, head_count, NOPE + ROPE
-    )
+    query_all = lax.optimization_barrier(jnp.dot(normed, full_query, preferred_element_type=f32))
+    query_all = query_all.reshape(length, head_count, NOPE + ROPE)
     query_rope = rotate(query_all[..., NOPE:], cosine[:, None, :], sine[:, None, :])
     queries = jnp.concatenate([query_all[..., :NOPE], query_rope], axis=-1).astype(bf16)
     latent_all = jnp.dot(normed, full_latent, preferred_element_type=f32)
@@ -865,11 +914,9 @@
     ffn_f, inverse_two = rms_forward(residual, gain_two)
     ffn_in = ffn_f.astype(bf16)
 
-    cot_half = rows_of(cotangent, core)
-    pieces = cut(0, half, GATHER_ORDERS, core_last=True) + cut(1, half, GATHER_ORDERS, core_last=True)
-    ffn_all, cot_all = gather(grid, [ffn_in, cot_half.astype(bf16)], [True, True], pieces, 2)
+    (ffn_all,) = gather(grid, [ffn_in], [True], cut(0, half, GATHER_ORDERS, core_last=True), 2)
     ffn_all = ffn_all.reshape(-1, width)
-    cot_all = cot_all.reshape(-1, width)
+    cot_right, ffn_all = all_rows(cot_bf[:, width // 2 :], ffn_all)
 
     routed = gates > 0.0
     triangle = (position[:, None] < position[None, :]).astype(bf16)
@@ -880,16 +927,13 @@
 
     def take(rows):
         return jnp.einsum(
-            "sct,std->scd", pick, rows.reshape(chips, length, width), preferred_element_type=f32
+            "sct,std->scd", pick, rows.reshape(chips, length, -1), preferred_element_type=f32
         )
 
-    def spread(rows):
-        return jnp.einsum(
-            "sct,scd->std", pick, rows.reshape(chips, capacity, width), preferred_element_type=f32
-        ).reshape(chips * length, width)
+    def spread(rows, units, weight):
+        return spread_rows(pick, rows.reshape(chips, capacity, width), units, weight)
 
     expert_rows = take(ffn_all).astype(bf16).reshape(-1, width)
-    grad_rows = (gate_slot * take(cot_all)).astype(bf16).reshape(-1, width)
     gate_rows = gate_slot.reshape(-1, 1)
     local_gate, local_up, local_down = expert_gate[0], expert_up[0], expert_down[0]
     gate_projected = jnp.dot(expert_rows, local_gate, preferred_element_type=f32)
@@ -897,17 +941,17 @@
     expert_hidden = (jax.nn.silu(gate_projected) * up_projected).astype(bf16)
     expert_part = jnp.dot(expert_hidden, local_down, preferred_element_type=f32)
     weighted = (gate_rows * expert_part).astype(bf16)
-    shared_g = jnp.dot(ffn_all, s_gate, preferred_element_type=f32)
-    shared_u = jnp.dot(ffn_all, s_up, preferred_element_type=f32)
+    shared_gu = jnp.dot(ffn_all, s_gate_up, preferred_element_type=f32)
+    shared_g, shared_u = shared_gu[:, :lanes], shared_gu[:, lanes:]
     shared_hidden = (jax.nn.silu(shared_g) * shared_u).astype(bf16)
-    shared_part = lax.dot_general(
-        shared_hidden, s_down_t, (((1,), (1,)), ((), ())), preferred_element_type=f32
-    )
-    forward_part = (shared_part + spread(weighted)).astype(bf16)
+    forward_part = spread(weighted, shared_hidden, s_down_t)
     block_shape = grid + (2, half, width)
     reduce_pieces = cut(0, half, REDUCE_ORDERS, core_first=True)
-    (ffn_total,) = reduce(grid, [forward_part.reshape(block_shape)], [True], reduce_pieces, 3)
-    output_half = (residual + ffn_total).astype(bf16)
+    forward_part, cot_left, cot_right = lax.optimization_barrier((forward_part, cot_left, cot_right))
+    grad_rows = jnp.concatenate(
+        [(gate_slot * take(part)).astype(bf16) for part in (cot_left, cot_right)], axis=-1
+    ).reshape(-1, width)
+    ffn_total = lax.psum_scatter(forward_part, ("dp", "tensor"), scatter_dimension=0, tiled=True)
 
     hidden_gradient = lax.dot_general(
         grad_rows, local_down, (((1,), (1,)), ((), ())), preferred_element_type=f32
@@ -917,40 +961,44 @@
     back_part = lax.dot_general(
         gate_gradient, local_gate, (((1,), (1,)), ((), ())), preferred_element_type=f32
     ) + lax.dot_general(up_gradient, local_up, (((1,), (1,)), ((), ())), preferred_element_type=f32)
-    shared_hg = jnp.dot(cot_all, s_down_t, preferred_element_type=f32)
-    grad_sgate = (shared_hg * shared_u * silu_slope(shared_g)).astype(bf16)
-    grad_sup = (shared_hg * jax.nn.silu(shared_g)).astype(bf16)
-    shared_back = lax.dot_general(
-        grad_sgate, s_gate, (((1,), (1,)), ((), ())), preferred_element_type=f32
-    ) + lax.dot_general(grad_sup, s_up, (((1,), (1,)), ((), ())), preferred_element_type=f32)
-    backward_part = (shared_back + spread(back_part.astype(bf16))).astype(bf16)
+    shared_hg = jnp.dot(cot_left, s_down_t[: width // 2], preferred_element_type=f32) + jnp.dot(
+        cot_right, s_down_t[width // 2 :], preferred_element_type=f32
+    )
+    grad_units = jnp.concatenate(
+        [shared_hg * shared_u * silu_slope(shared_g), shared_hg * jax.nn.silu(shared_g)], axis=1
+    ).astype(bf16)
+    backward_part = spread(back_part.astype(bf16), grad_units, s_gate_up)
     (grad_ffn,) = reduce(grid, [backward_part.reshape(block_shape)], [True], reduce_pieces, 3)
 
     grad_expert_down = jnp.dot(expert_hidden.T, grad_rows, preferred_element_type=f32)
     grad_expert_gate = jnp.dot(expert_rows.T, gate_gradient, preferred_element_type=f32)
     gradient_expert_upward = jnp.dot(expert_rows.T, up_gradient, preferred_element_type=f32)
-    shared_grads = jnp.stack(
-        [
-            jnp.dot(ffn_all.T, grad_sgate, preferred_element_type=f32),
-            jnp.dot(ffn_all.T, grad_sup, preferred_element_type=f32),
-            jnp.dot(cot_all.T, shared_hidden, preferred_element_type=f32),
-        ]
-    ).astype(bf16)
+    over_rows = (((0,), (0,)), ((), ()))
+    down_parts = [
+        lax.dot_general(shared_hidden, part, over_rows, preferred_element_type=f32).astype(bf16)
+        for part in (cot_left, cot_right)
+    ]
+    unit_grads = lax.dot_general(grad_units, ffn_all, over_rows, preferred_element_type=f32)
+    unit_grads, *down_parts = lax.optimization_barrier((unit_grads.astype(bf16), *down_parts))
+    shared_grads = jnp.concatenate([unit_grads, jnp.concatenate(down_parts, axis=1)])
     returned = lax.all_to_all(
-        shared_grads.reshape(3, chips, model_rows, part_units).transpose(1, 0, 2, 3),
+        shared_grads.reshape(3 * lanes, chips, model_rows).transpose(1, 0, 2),
         "dp",
         split_axis=0,
         concat_axis=0,
         tiled=True,
-    )
-    returned = returned.transpose(1, 2, 0, 3).reshape(3, model_rows, -1).astype(f32)
-    s_sgate, s_sup, s_sdown = returned[0], returned[1], returned[2].T
+    ).astype(f32)
+    s_sgate, s_sup, s_sdown = (
+        returned[:, i * lanes : i * lanes + part_units].reshape(-1, model_rows) for i in range(3)
+    )
+    s_sgate, s_sup = s_sgate.T, s_sup.T
 
     grad_res_part, g_fgain = rms_backward(residual, inverse_two, gain_two, grad_ffn)
     grad_residual = cot_half + grad_res_part
     (grad_attn,) = pair(grid, [grad_residual.astype(bf16)], True, 6)
     grad_attn = grad_attn.reshape(length, width)
     g_out_t = jnp.dot(grad_attn.T, context, preferred_element_type=f32)
+    s_out_t = lax.psum_scatter(g_out_t.astype(bf16), "dp", scatter_dimension=0, tiled=True)
     grad_context = (
         jnp.dot(grad_attn, full_out_t, preferred_element_type=f32)
         .astype(bf16)
@@ -1013,21 +1061,22 @@
     g_gains = jnp.pad(g_gains[:, None, :], ((0, 0), (0, 15), (0, 0)))
     terms = [
         g_query.astype(bf16).reshape(grid + (-1, g_query.shape[1])),
-        g_out_t.astype(bf16).reshape(grid + (-1, g_out_t.shape[1])),
         g_up.astype(bf16).reshape(grid + (-1, g_up.shape[1])),
         g_latent.astype(bf16).reshape(grid + (2, -1, g_latent.shape[1])),
         g_gains.astype(bf16).reshape(grid + (16, -1)),
     ]
     pieces = (
-        cut(0, terms[0].shape[-2], REDUCE_COARSE)
-        + cut(1, terms[1].shape[-2], REDUCE_COARSE)
-        + cut(2, terms[2].shape[-2], ((1, (X, Y, Z)), (1, (Y, X, Z))))
-        + cut(3, terms[3].shape[-2], ((1, (Z, X, Y)),), core_first=True)
-        + cut(4, terms[4].shape[-2], ((1, (X, Y, Z)),))
-    )
-    s_query, s_out_t, s_up, latent_half, gain_sums = reduce(
-        grid, terms, [False, False, False, True, False], pieces, 4
-    )
+        cut(0, terms[0].shape[-2], REDUCE_ORDERS)
+        + cut(1, terms[1].shape[-2], ((1, (X, Y, Z)), (1, (Y, X, Z))))
+        + cut(2, terms[2].shape[-2], ((1, (Z, X, Y)),), core_first=True)
+        + cut(3, terms[3].shape[-2], ((1, (X, Y, Z)),))
+    )
+    s_query, s_up, latent_half, gain_sums = reduce(
+        grid, terms, [False, False, True, False], pieces, 4
+    )
+    ffn_total, s_out_t, gain_sums = lax.optimization_barrier((ffn_total, s_out_t, gain_sums))
+    s_out_t = s_out_t.astype(f32)
+    output_half = (residual + ffn_total.astype(f32)).astype(bf16)
     output, grad_input, s_latent, gain_sums = pair(
         grid, [output_half, grad_input_half, latent_half, gain_sums], True, 8
     )

time: 1120 us -> 1020 us (0.911)
  waiting for transfers between devices: 0.01 us -> 142 us
  matrix products: 304 us -> 191 us
  Pallas kernels: 622 us -> 535 us
  local copies, waits for them, and re-layouts: 131 us -> 77.3 us
  between operations: 2.29 us -> 15.8 us
    dot_general x13 -> x9, matrix products: 165 us -> 48.7 us  [the longest x3 15.2 us: take(): jnp.einsum('sct,std->scd', pick, rows.reshape(chips, length, -1), preferr...]
    all_gather x0 -> x2, waiting for transfers between devices: none -> 88.4 us  [all_rows(): return (lax.all_gather(part, ('dp', 'tensor'), axis=0, tiled=True), after)]
    pallas_call x2, Pallas kernels: 274 us -> 210 us  [gather(): pl.pallas_call(functools.partial(gather_body, grid, pieces, shared_flags,...]
    pallas_call x3 -> x2, Pallas kernels: 336 us -> 282 us  [reduce(): pl.pallas_call(functools.partial(reduce_body, grid, pieces, shared_flags,...]
    dot_general x3 -> x0, local copies, waits for them, and re-layouts: 51.2 us -> none  [the longest x1 21.6 us: dense_shards(): jnp.dot(ffn_all.T, grad_sgate, preferred_element_type=f32)]
    reduce_scatter x0 -> x2, waiting for transfers between devices: none -> 46.9 us  [the longest x1 46.9 us: dense_shards(): lax.psum_scatter(forward_part, ('dp', 'tensor'), scatter_dimension=0, til...]
    pallas_call x0 -> x2, Pallas kernels: none -> 29.2 us  [spread_rows(): pl.pallas_call(spread_body, grid=(count,), out_shape=jax.ShapeDtypeStruct...]
    unnamed x237 -> x241, local copies, waits for them, and re-layouts: 48.8 us -> 47.3 us
  transfers between devices with their start and end apart: 2 -> 6, of which waited for: 0 -> 4; matrix products, arithmetic and copies ran while one was open for 25% -> 16% of each run, Pallas kernels for 41% -> 21%
where the time goes in v2:
time: 1020 us; the launch traced here: 1010 us
  Pallas kernels  535 us (52%)
  matrix products  191 us (19%)
  waiting for transfers between devices  142 us (14%)
  local copies, waits for them, and re-layouts  77.3 us (8%)
  other arithmetic  40.9 us (4%)
  between operations  15.8 us (2%)
  starting transfers between devices  10.4 us (1%)
    pallas_call x2, Pallas kernels, reduce(): pl.pallas_call(functools.partial(reduce_body, grid, pieces, shared_flags,...  282 us
    pallas_call x2, Pallas kernels, gather(): pl.pallas_call(functools.partial(gather_body, grid, pieces, shared_flags,...  210 us
    all_gather x2, waiting for transfers between devices, all_rows(): return (lax.all_gather(part, ('dp', 'tensor'), axis=0, tiled=True), after)  88.4 us
    unnamed x241, local copies, waits for them, and re-layouts  47.3 us
    reduce_scatter x1, waiting for transfers between devices, dense_shards(): lax.psum_scatter(forward_part, ('dp', 'tensor'), scatter_dimension=0, til...  46.9 us
    pallas_call x2, Pallas kernels, spread_rows(): pl.pallas_call(spread_body, grid=(count,), out_shape=jax.ShapeDtypeStruct...  29.2 us
  transfers between devices with their start and end apart: 6, of which 4 were waited for; matrix products, arithmetic and copies ran while one was open for 16% of the time, Pallas kernels for 21%

profile of v2, /device:TPU:0, one launch (start us, length us, event | category | flops | bytes accessed | tf_op | source)
XLA Modules:
  0.0 1012.2 jit_solution(17251666655268678998)
XLA Ops:
  14.7 123.0 %gather_rows.2 = (bf16[4,2,2,128,1536]{4,3,2,1,0:T(8,128)(2,1)S(1)}, bf16[4,2,2,128,1024]{4,3,2,1,0:T(8,128)(2,1)S(1)}, bf16[4,2,2,32,2048]{4,3,2,1,0:T(8,128)(2...) custom-call(bf16[128,1536]{1,0:T(8,128)(2,1)S(1)} %copy-done.17, ...), custom_call_target="tpu_custom_call" | custom-call | tf_op jit(solution)/shard_map/gather_rows/pallas_call | solution.py:500
  140.5 2.7 copy-done.21
  143.2 2.0 copy-done.22
  146.9 2.9 convert_element_type.160
  153.6 6.1 fusion.100
  159.7 3.0 copy.142
  162.8 3.5 convolution_convert_fusion.6
  166.3 2.3 copy.184
  177.3 2.6 fusion.101
  181.2 2.7 pair_rows.4
  184.9 3.0 multiply_reduce_fusion.6
  191.9 87.1 %gather_rows.3 = bf16[4,2,2,2,128,2048]{5,4,3,2,1,0:T(8,128)(2,1)S(1)} custom-call(bf16[128,2048]{1,0:T(8,128)(2,1)S(1)} %multiply_convert_fusion.11.refs_0_), custom_call_target="tpu_custom_call" | custom-call | tf_op jit(solution)/shard_map/gather_rows/pallas_call | solution.py:500
  279.1 5.7 copy-done.2
  285.6 1.9 copy.152
  287.5 1.9 copy.153
  289.4 2.6 fusion.33
  292.0 4.6 all-to-all-start
  296.8 8.1 convolution_convert_fusion.1
  305.0 9.6 fusion.14
  314.7 8.4 multiply_convert_fusion.5
  325.0 9.8 multiply_convert_fusion
  334.8 5.6 all-to-all-done
  340.4 2.6 copy.154
  344.2 2.4 slice.247.weight_ref
  346.7 8.6 fusion.90
  357.3 14.5 %spread_rows.2 = bf16[4096,2048]{1,0:T(8,128)(2,1)} custom-call(bf16[16,112,256]{2,1,0:T(8,128)(2,1)S(1)} %copy-done.5, bf16[16,112,2048]{2,1,0:T(8,128)(2,1)S(1)} %bitcast.194, bf16[4096,128]{1,0:T(8,128)(2,1)S(1)} %multiply_convert_fusion.9.units_ref, bf16[2048,128]{1,0:T(8,128)(2,1)S(1)} %slice.250.weight_ref), custom_call_target="tpu_custom_call" | custom-call | flops 4026531840 | bytes 24117248 | tf_op jit(solution)/shard_map/spread_rows/pallas_call | solution.py:769
  372.9 9.3 all-gather.5.cloned.1.call-done
  382.2 79.1 %all-gather.3.cloned.1.call-done = bf16[4096,1024]{1,0:T(8,128)(2,1)} async-done(((bf16[128,1024]{1,0:T(8,128)(2,1)}), bf16[4096,1024]{1,0:T(8,128)(2,1)}) %all-gather.3.cloned.1.call-update) | async-done | bytes 8388624 | tf_op jit(solution)/shard_map/all_gather | solution.py:870
  461.3 6.0 fusion.56
  467.3 3.5 multiply_convert_fusion.2
  472.3 4.7 multiply_convert_fusion.8
  477.0 3.5 multiply_convert_fusion.1
  480.6 7.4 pad_maximum_fusion
  487.9 11.6 %multiply_convert_fusion.3 = (bf16[1792,704]{0,1:T(8,128)(2,1)S(1)}, bf16[1792,704]{0,1:T(8,128)(2,1)S(1)}) fusion(f32[1792,704]{0,1:T(8,128)} %copy-done.96, f32[1792,704]{0,1:T(8,128)} %get-tuple-element.194, bf16[1792,2048]{1,0:T(8,128)(2,1)} %bitcast.231, bf16[1,704,2048]{2,1,0:T(8,128)(2,1)S(1)} %copy-done), kind=kOutput, calls=%fused_computation.7 | convolution fusion | flops 5183782912 | bytes 25362432 | tf_op jit(solution)/shard_map/dot_general | solution.py:956
  499.6 9.5 fusion.12
  510.9 9.5 add_convert_fusion
  520.4 14.6 %spread_rows.3 = bf16[4096,2048]{1,0:T(8,128)(2,1)} custom-call(bf16[16,112,256]{2,1,0:T(8,128)(2,1)S(1)} %copy-done.6, bf16[16,112,2048]{2,1,0:T(8,128)(2,1)S(1)} %bitcast.195, bf16[4096,256]{1,0:T(8,128)(2,1)S(1)} %pad_maximum_fusion.1.units_ref, bf16[2048,256]{1,0:T(8,128)(2,1)S(1)} %copy-done.7), custom_call_target="tpu_custom_call" | custom-call | flops 6174015488 | bytes 24117248 | tf_op jit(solution)/shard_map/spread_rows/pallas_call | solution.py:769
  535.1 82.6 %reduce_rows.2 = f32[128,2048]{1,0:T(8,128)} custom-call(bf16[4,2,2,2,128,2048]{5,4,3,2,1,0:T(8,128)(2,1)} %bitcast.216), custom_call_target="tpu_custom_call" | custom-call | tf_op jit(solution)/shard_map/reduce_rows/pallas_call | solution.py:680
  619.4 2.7 fusion.92
  622.0 1.9 pair_rows.5
  624.0 3.3 convolution_convert_fusion.2
  628.7 4.8 convolution_convert_fusion.10
  633.5 4.9 convolution_convert_fusion.9
  640.2 4.5 convolution_convert_fusion.5
  646.3 5.5 all-to-all-start.1
  651.8 4.3 convolution_convert_fusion.8
  659.3 4.9 fusion.37
  666.5 5.1 fusion.34
  672.8 2.3 convolution_bitcast_fusion.3
  678.5 4.6 fusion.103
  683.3 3.2 pair_rows.6
  687.1 4.5 multiply_reduce_fusion.2
  693.1 2.7 copy.168
  695.9 6.0 convolution_convert_fusion
  701.9 10.7 %convolution_bitcast_fusion.2 = f32[1,704,2048]{2,1,0:T(8,128)} fusion(bf16[1792,704]{0,1:T(8,128)(2,1)S(1)} %copy-done.101, bf16[1792,2048]{1,0:T(8,128)(2,1)} %bitcast.232), kind=kOutput, calls=%fused_computation.19 | convolution fusion | flops 5167382528 | bytes 15630336 | tf_op jit(solution)/shard_map/dot_general | solution.py:973
  712.6 7.1 convolution_bitcast_fusion
  719.8 2.2 convolution_convert_fusion.4
  722.0 199.4 %reduce_rows.3 = (f32[128,1536]{1,0:T(8,128)}, f32[32,2048]{1,0:T(8,128)}, f32[64,576]{1,0:T(8,128)}, f32[16,384]{1,0:T(8,128)}) custom-call(bf16[4,2,2,128,1536]{4,3,2,1,0:T(8,128)(2,1)} %bitcast.217, bf16[4,2,2,32,2048]{4,3,2,1,0:T(8,128)(2,1)} %bitcast.225, bf16[4,2,2,2,64,576]{5,4,3,2,1,0:T(8,128)(2,1)} %bitcast.224, bf16[4,2,2,16,384]{4,3,2,1,0:T(8,128)(2,1)} %bitcast.248), custom_call_target="tpu_custom_call" | custom-call | tf_op jit(solution)/shard_map/reduce_rows/pallas_call | solution.py:680
  921.4 2.7 subtract_add_fusion.refs_1_
  924.1 10.3 %convolution_bitcast_fusion.1 = f32[1,2048,704]{1,2,0:T(8,128)} fusion(bf16[1792,704]{0,1:T(8,128)(2,1)S(1)} %copy-done.100, bf16[1792,2048]{1,0:T(8,128)(2,1)} %bitcast.220), kind=kOutput, calls=%fused_computation.18 | convolution fusion | flops 5167382528 | bytes 15630336 | tf_op jit(solution)/shard_map/dot_general | solution.py:974
  934.4 2.2 fusion.93
  938.9 46.9 %reduce-scatter.3.cloned.1.call-done = bf16[128,2048]{1,0:T(8,128)(2,1)} async-done(((bf16[4096,2048]{1,0:T(8,128)(2,1)}), bf16[128,2048]{1,0:T(8,128)(2,1)}) %reduce-scatter.3.cloned.1.call-update) | async-done | bytes 524304 | tf_op jit(solution)/shard_map/reduce_scatter | solution.py:954
  988.2 6.0 pair_rows.7
  1000.4 3.3 copy.207
  (328 shorter events, 71.5 us)
Async XLA Ops:
  7.2 317.8 %copy-start = (bf16[1,704,2048]{2,1,0:T(8,128)(2,1)S(1)}, bf16[1,704,2048]{2,1,0:T(8,128)(2,1)}, u32[]{:S(2)}) copy-start(bf16[1,704,2048]{2,1,0:T(8,128)(2,1)} %param.31) | copy-start | bytes 8650756
  7.2 375.0 %all-gather.5.cloned.1.call-start = ((), (), s32[]{:S(2)}) async-start(), calls=%async_computation.5 | async-start | bytes 8650752 | tf_op jit(solution)/shard_map/all_gather | solution.py:870
  145.3 4.6 copy-start.65
  145.3 45.2 %copy-start.67 = (f32[2048]{0:T(1024)}, f32[2048]{0:T(1024)S(1)}, u32[]{:S(2)}) copy-start(f32[2048]{0:T(1024)S(1)} %get-tuple-element.50) | copy-start | bytes 24580
  145.3 4.6 copy-start.29
  153.5 18.6 %copy-start.59 = (f32[256,32]{0,1:T(8,128)}, f32[256,32]{0,1:T(8,128)S(1)}, u32[]{:S(2)}) copy-start(f32[256,32]{0,1:T(8,128)S(1)} %copy.144) | copy-start | bytes 98308
  162.7 5.9 copy-start.77
  162.8 5.8 copy-start.75
  166.3 4.2 copy-start.62
  166.3 5.7 copy-start.87
  188.4 90.6 %copy-start.84 = (f32[128]{0:T(128)}, f32[128]{0:T(128)S(1)}, u32[]{:S(2)}) copy-start(f32[128]{0:T(128)S(1)} %get-tuple-element.186) | copy-start | bytes 1540
  279.1 5.7 copy-start.2
  284.8 176.5 %all-gather.3.cloned.1.call-start = ((), (), s32[]{:S(2)}) async-start(), calls=%async_computation.4 | async-start | bytes 8650752 | tf_op jit(solution)/shard_map/all_gather | solution.py:870
  292.0 48.4 %all-to-all-start = ((bf16[16,128,384]{1,2,0:T(8,128)(2,1)}), bf16[16,128,384]{1,2,0:T(8,128)(2,1)}, u32[]{:S(2)}, u32[]{:S(2)}) async-start(bf16[16,128,384]{1,2,0:T(8,128)(2,1)} %fusion.33), calls=%async_computation | async-start | bytes 3145728 | tf_op jit(solution)/shard_map/all_to_all | solution.py:835
  296.6 642.3 %reduce-scatter.5.cloned.1.call-start = ((), (), s32[]{:S(2)}) async-start(), calls=%async_computation.7 | async-start | bytes 4456448 | tf_op jit(solution)/shard_map/reduce_scatter | solution.py:1001
  305.0 9.7 copy-start.27
  305.0 9.7 copy-start.93
  314.7 8.5 copy-start.96
  343.0 3.6 copy-start.33
  344.2 13.1 %slice-start.4 = ((s8[7340032]{0:T(1024)(128)(4,1)}), s8[4194304]{0:T(1024)(128)(4,1)S(1)}, s32[]{:S(2)}) async-start(s8[7340032]{0:T(1024)(128)(4,1)} %bitcast.192), calls=%async_computation.12 | async-start | bytes 8388608
  346.7 10.7 %slice-start.5 = ((s8[7340032]{0:T(1024)(128)(4,1)}), s8[3145728]{0:T(1024)(128)(4,1)S(1)}, s32[]{:S(2)}) async-start(s8[7340032]{0:T(1024)(128)(4,1)} %bitcast.192), calls=%async_computation.13 | async-start | bytes 6291456
  461.3 6.0 copy-start.24
  461.3 9.5 slice-start.6
  467.3 5.0 copy-start.37
  477.0 32.0 %copy-start.46 = (bf16[4096,128]{1,0:T(8,128)(2,1)}, bf16[4096,128]{1,0:T(8,128)(2,1)S(1)}, u32[]{:S(2)}) copy-start(bf16[4096,128]{1,0:T(8,128)(2,1)S(1)} %get-tuple-element.149) | copy-start | bytes 3145732
  487.9 11.7 %copy-start.92 = (bf16[1,2048,704]{1,2,0:T(8,128)(2,1)S(1)}, bf16[1,2048,704]{1,2,0:T(8,128)(2,1)}, u32[]{:S(2)}) copy-start(bf16[1,2048,704]{1,2,0:T(8,128)(2,1)} %param.29) | copy-start | bytes 8650756
  499.6 9.5 copy-start.99
  499.6 9.8 copy-start.97
  499.6 9.5 copy-start.48
  510.9 9.5 copy-start.6
  510.9 9.5 copy-start.7
  535.1 82.6 %copy-start.25 = (f32[128,2048]{1,0:T(8,128)S(1)}, f32[128,2048]{1,0:T(8,128)}, u32[]{:S(2)}) copy-start(f32[128,2048]{1,0:T(8,128)} %get-tuple-element.146) | copy-start | bytes 3145732
  535.1 82.6 %copy-start.68 = (f32[2048]{0:T(1024)S(1)}, f32[2048]{0:T(1024)}, u32[]{:S(2)}) copy-start(f32[2048]{0:T(1024)} %copy-done.67) | copy-start | bytes 24580
  535.1 82.7 %copy-start.85 = (f32[128]{0:T(128)S(1)}, f32[128]{0:T(128)}, u32[]{:S(2)}) copy-start(f32[128]{0:T(128)} %copy-done.84) | copy-start | bytes 1540
  619.4 4.6 copy-start.53
  627.3 358.4 %reduce-scatter.3.cloned.1.call-start = ((), (), s32[]{:S(2)}) async-start(), calls=%async_computation.6 | async-start | bytes 17301504 | tf_op jit(solution)/shard_map/reduce_scatter | solution.py:954
  628.7 9.8 slice-start
  628.7 9.8 slice-start.1
  633.5 5.0 slice-start.2
  633.5 6.2 slice-start.3
  633.5 6.4 copy-start.47
  633.5 6.7 copy-start.49
  646.3 288.1 %all-to-all-start.1 = ((bf16[16,384,128]{2,1,0:T(8,128)(2,1)}), bf16[16,384,128]{2,1,0:T(8,128)(2,1)}, u32[]{:S(2)}, u32[]{:S(2)}) async-start(bf16[16,384,128]{2,1,0:T(8,128)(2,1)} %bitcast_bitcast_fusion), calls=%async_computation.3 | async-start | bytes 3145728 | tf_op jit(solution)/shard_map/all_to_all | solution.py:984
  651.8 5.7 copy-start.39
  666.5 6.3 copy-start.74
  683.2 3.7 copy-start.88
  683.3 3.7 copy-start.66
  683.3 3.7 copy-start.86
  687.1 5.2 copy-start.32
  695.9 6.1 copy-start.101
  695.9 16.7 %slice-start.8 = ((s8[7340032]{0:T(1024)(128)(4,1)}), s8[3145728]{0:T(1024)(128)(4,1)S(1)}, s32[]{:S(2)}) async-start(s8[7340032]{0:T(1024)(128)(4,1)} %bitcast.221), calls=%async_computation.16 | async-start | bytes 6291456
  701.9 10.7 %slice-start.9 = ((s8[7340032]{0:T(1024)(128)(4,1)}), s8[4194304]{0:T(1024)(128)(4,1)S(1)}, s32[]{:S(2)}) async-start(s8[7340032]{0:T(1024)(128)(4,1)} %bitcast.221), calls=%async_computation.17 | async-start | bytes 8388608
  701.9 10.7 %copy-start.98 = (bf16[1792,704]{0,1:T(8,128)(2,1)S(1)}, bf16[1792,704]{0,1:T(8,128)(2,1)}, u32[]{:S(2)}) copy-start(bf16[1792,704]{0,1:T(8,128)(2,1)} %copy-done.97) | copy-start | bytes 7569412
  712.6 7.2 copy-start.35
  712.6 7.2 copy-start.41
  722.0 199.5 %copy-start.28 = (f32[256,2048]{1,0:T(8,128)S(1)}, f32[256,2048]{1,0:T(8,128)}, u32[]{:S(2)}) copy-start(f32[256,2048]{1,0:T(8,128)} %convert_element_type.160) | copy-start | bytes 6291460
  722.0 199.5 %copy-start.42 = (f32[128,2048]{1,0:T(8,128)S(1)}, f32[128,2048]{1,0:T(8,128)}, u32[]{:S(2)}) copy-start(f32[128,2048]{1,0:T(8,128)} %get-tuple-element.144) | copy-start | bytes 3145732
  722.0 199.5 %copy-start.90 = (f32[128]{0:T(128)S(1)}, f32[128]{0:T(128)}, u32[]{:S(2)}) copy-start(f32[128]{0:T(128)} %get-tuple-element.196) | copy-start | bytes 1540
  936.7 49.1 %copy-start.26 = (f32[128,2048]{1,0:T(8,128)S(1)}, f32[128,2048]{1,0:T(8,128)}, u32[]{:S(2)}) copy-start(f32[128,2048]{1,0:T(8,128)} %get-tuple-element.146) | copy-start | bytes 3145732
  937.8 49.2 %copy-start.18 = (f32[64,576]{1,0:T(8,128)S(1)}, f32[64,576]{1,0:T(8,128)}, u32[]{:S(2)}) copy-start(f32[64,576]{1,0:T(8,128)} %get-tuple-element.61.refs_2_) | copy-start | bytes 442372
  937.8 49.2 %copy-start.20 = (f32[16,384]{1,0:T(8,128)S(1)}, f32[16,384]{1,0:T(8,128)}, u32[]{:S(2)}) copy-start(f32[16,384]{1,0:T(8,128)} %get-tuple-element.62.refs_3_) | copy-start | bytes 73732
  985.8 12.6 %copy-start.61 = (bf16[128,1024]{1,0:T(8,128)(2,1)S(1)}, bf16[128,1024]{1,0:T(8,128)(2,1)}, u32[]{:S(2)}) copy-start(bf16[128,1024]{1,0:T(8,128)(2,1)} %reduce-scatter.5.cloned.1.call-done) | copy-start | bytes 786436
  1000.4 4.2 copy-start.64
  1000.4 4.9 copy-start.1
  (54 other events, 98.8 us)
Sparse Core Ops, SparseCore 0:
  284.9 97.1 all-gather.4
  385.6 75.6 all-gather.2
  627.4 124.8 reduce-scatter.4
  754.5 231.2 reduce-scatter.2

commit v3 on v2

--- a/solution.py
+++ b/solution.py
@@ -6,6 +6,7 @@
 from jax.experimental import pallas as pl
 from jax.experimental.pallas import tpu as pltpu
 from jax.sharding import PartitionSpec as P
+
 
 NOPE = 128
 ROPE = 64
@@ -383,7 +384,7 @@
     pl.semaphore_wait(barrier, peers)
 
 
-def stage_plan(sizes, order, weight, first):
+def stage_plan(sizes, order, weight):
     plan, now, held = [], 0.0, 1
     for dim in order:
         for step in range(sizes[dim] - 1):
@@ -402,15 +403,15 @@
     send_sem, recv_sem, own_sem = refs[2 * input_count :]
     place = place_of(grid)
 
-    def window(number, piece, chosen):
-        which, start, rows, order = piece
+    def window(piece, chosen):
+        which, start, rows, _ = piece
         spots = tuple(chosen.get(dim, place[dim]) for dim in range(4 if shared_flags[which] else 3))
         return outputs[which].at[spots + (pl.ds(start, rows),)]
 
     own = []
     for number, piece in enumerate(pieces):
         which, start, rows, order = piece
-        copy = pltpu.make_async_copy(inputs[which].at[pl.ds(start, rows)], window(number, piece, {}), own_sem.at[number])
+        copy = pltpu.make_async_copy(inputs[which].at[pl.ds(start, rows)], window(piece, {}), own_sem.at[number])
         copy.start()
         own.append(copy)
     greet(grid, place)
@@ -419,12 +420,11 @@
     for number, piece in enumerate(pieces):
         which, start, rows, order = piece
         weight = rows * inputs[which].shape[1]
-        for rank, (when, dim, step) in enumerate(stage_plan(sizes, order, weight, 0.0)):
+        for rank, (when, dim, step) in enumerate(stage_plan(sizes, order, weight)):
             stages.append((when, number, rank, dim, step))
     stages.sort(key=lambda s: s[:3])
     pending_recv = {number: [] for number in range(len(pieces))}
     sends = []
-    slot_of = {}
 
     def copies(number, rank, dim, step):
         piece = pieces[number]
@@ -436,7 +436,7 @@
         made = []
         base = 2 * rank
         if size == 2:
-            part = window(number, piece, gathered)
+            part = window(piece, gathered)
             if not gathered:
                 source = inputs[which].at[pl.ds(start, rows)]
             else:
@@ -455,7 +455,7 @@
             arrives = (back >= 0) & (back < size) & (back_block >= 0) & (back_block < size)
             chosen = dict(gathered)
             chosen[dim] = jnp.clip(block, 0, size - 1)
-            part = window(number, piece, chosen)
+            part = window(piece, chosen)
             if not gathered and step == 0:
                 source = inputs[which].at[pl.ds(start, rows)]
             else:
@@ -586,7 +586,6 @@
     stages = []
     for number, (which, start, rows, order) in enumerate(pieces):
         weight = rows * inputs[which].shape[-1]
-        slot = 0
         for rank, (when, dim, step) in enumerate(reduce_plan(sizes, order, weight)):
             stages.append((when, number, rank, dim, step))
     stages.sort(key=lambda s: s[:3])
@@ -596,7 +595,6 @@
 
     for when, number, rank, dim, step in stages:
         which, start, rows, order = pieces[number]
-        width = inputs[which].shape[-1]
         dims = 4 if shared_flags[which] else 3
         if rank == 0:
             loads[number].wait()
@@ -914,6 +912,7 @@
     ffn_f, inverse_two = rms_forward(residual, gain_two)
     ffn_in = ffn_f.astype(bf16)
 
+    ffn_in, cot_left = lax.optimization_barrier((ffn_in, cot_left))
     (ffn_all,) = gather(grid, [ffn_in], [True], cut(0, half, GATHER_ORDERS, core_last=True), 2)
     ffn_all = ffn_all.reshape(-1, width)
     cot_right, ffn_all = all_rows(cot_bf[:, width // 2 :], ffn_all)
@@ -998,7 +997,8 @@
     (grad_attn,) = pair(grid, [grad_residual.astype(bf16)], True, 6)
     grad_attn = grad_attn.reshape(length, width)
     g_out_t = jnp.dot(grad_attn.T, context, preferred_element_type=f32)
-    s_out_t = lax.psum_scatter(g_out_t.astype(bf16), "dp", scatter_dimension=0, tiled=True)
+    g_out_t, ffn_total = lax.optimization_barrier((g_out_t.astype(bf16), ffn_total))
+    s_out_t = lax.psum_scatter(g_out_t, "dp", scatter_dimension=0, tiled=True)
     grad_context = (
         jnp.dot(grad_attn, full_out_t, preferred_element_type=f32)
         .astype(bf16)

time: 1020 us -> 1010 us (level)
  waiting for transfers between devices: 142 us -> 73.8 us
  Pallas kernels: 535 us -> 567 us
  matrix products: 191 us -> 205 us
    all_gather x2, waiting for transfers between devices: 88.4 us -> 30.4 us  [all_rows(): return (lax.all_gather(part, ('dp', 'tensor'), axis=0, tiled=True), after)]
    reduce_scatter x1, waiting for transfers between devices: 46.9 us -> 0.01 us  [dense_shards(): lax.psum_scatter(forward_part, ('dp', 'tensor'), scatter_dimension=0, til...]
    all_to_all x1, waiting for transfers between devices: 5.62 us -> 43.3 us  [dense_shards(): lax.all_to_all(stacked, 'dp', split_axis=0, concat_axis=0, tiled=True)]
    pallas_call x2, Pallas kernels: 282 us -> 316 us  [reduce(): pl.pallas_call(functools.partial(reduce_body, grid, pieces, shared_flags,...]
    dot_general x1, matrix products: 8.44 us -> 19.5 us  [dense_shards(): up_projected = jnp.dot(expert_rows, local_up, preferred_element_type=f32)]
    unnamed x241 -> x237, local copies, waits for them, and re-layouts: 47.3 us -> 47.5 us
  transfers between devices with their start and end apart: 6 -> 6, of which waited for: 4 -> 2; matrix products, arithmetic and copies ran while one was open for 16% -> 28% of each run, Pallas kernels for 21% -> 35%
where the time goes in v3:
time: 1010 us; the launch traced here: 997 us
  Pallas kernels  567 us (56%)
  matrix products  205 us (20%)
  local copies, waits for them, and re-layouts  83.1 us (8%)
  waiting for transfers between devices  73.8 us (7%)
  other arithmetic  35.4 us (4%)
  starting transfers between devices  17.2 us (2%)
  between operations  15.7 us (2%)
    pallas_call x2, Pallas kernels, reduce(): pl.pallas_call(functools.partial(reduce_body, grid, pieces, shared_flags,...  316 us
    pallas_call x2, Pallas kernels, gather(): pl.pallas_call(functools.partial(gather_body, grid, pieces, shared_flags,...  210 us
    unnamed x237, local copies, waits for them, and re-layouts  47.5 us
    all_to_all x1, waiting for transfers between devices, dense_shards(): lax.all_to_all(stacked, 'dp', split_axis=0, concat_axis=0, tiled=True)  43.3 us
    all_gather x2, waiting for transfers between devices, all_rows(): return (lax.all_gather(part, ('dp', 'tensor'), axis=0, tiled=True), after)  30.4 us
    pallas_call x2, Pallas kernels, spread_rows(): pl.pallas_call(spread_body, grid=(count,), out_shape=jax.ShapeDtypeStruct...  29 us
    dot_general x3, matrix products, take(): jnp.einsum('sct,std->scd', pick, rows.reshape(chips, length, -1), preferr...  25.3 us
  transfers between devices with their start and end apart: 6, of which 2 were waited for; matrix products, arithmetic and copies ran while one was open for 28% of the time, Pallas kernels for 35%

profile of v3, /device:TPU:0, one launch (start us, length us, event | category | flops | bytes accessed | tf_op | source)
XLA Modules:
  0.0 996.9 jit_solution(2593093729669574425)
XLA Ops:
  14.0 123.0 %gather_rows.2 = (bf16[4,2,2,128,1536]{4,3,2,1,0:T(8,128)(2,1)S(1)}, bf16[4,2,2,128,1024]{4,3,2,1,0:T(8,128)(2,1)S(1)}, bf16[4,2,2,32,2048]{4,3,2,1,0:T(8,128)(2...) custom-call(bf16[128,1536]{1,0:T(8,128)(2,1)S(1)} %copy-done.20, ...), custom_call_target="tpu_custom_call" | custom-call | tf_op jit(solution)/shard_map/gather_rows/pallas_call | solution.py:500
  140.7 2.7 copy-done.25
  143.4 2.0 copy-done.26
  148.3 2.9 convert_element_type.160
  158.7 6.1 fusion.100
  164.8 3.0 copy.142
  169.4 3.3 convolution_convert_fusion.6
  172.7 2.3 copy.184
  178.7 2.1 slice.324
  182.1 1.9 fusion.31
  185.5 1.8 copy-done.27
  188.7 2.7 pair_rows.4
  192.9 30.4 %all-gather.3.cloned.1.call-done = bf16[4096,1024]{1,0:T(8,128)(2,1)} async-done(((bf16[128,1024]{1,0:T(8,128)(2,1)}), bf16[4096,1024]{1,0:T(8,128)(2,1)}) %all-gather.3.cloned.1.call-update) | async-done | bytes 8388624 | tf_op jit(solution)/shard_map/all_gather | solution.py:868
  223.3 87.1 %gather_rows.3 = bf16[4,2,2,2,128,2048]{5,4,3,2,1,0:T(8,128)(2,1)S(1)} custom-call(bf16[128,2048]{1,0:T(8,128)(2,1)S(1)} %multiply_convert_fusion.11.refs_0_), custom_call_target="tpu_custom_call" | custom-call | tf_op jit(solution)/shard_map/gather_rows/pallas_call | solution.py:500
  310.5 5.7 copy-done.2
  317.4 1.9 copy.153
  319.3 2.5 fusion.33
  321.8 4.4 all-to-all-start
  329.2 43.3 %all-to-all-done = bf16[16,128,384]{1,2,0:T(8,128)(2,1)} async-done(((bf16[16,128,384]{1,2,0:T(8,128)(2,1)}), bf16[16,128,384]{1,2,0:T(8,128)(2,1)}, u32[]{:S(2)}, u32[]{:S(2)}) %all-to-all-start) | async-done | bytes 1572896 | tf_op jit(solution)/shard_map/all_to_all | solution.py:833
  372.5 2.7 copy.154
  376.2 8.9 fusion.90
  387.1 11.6 %convolution_convert_fusion.1 = bf16[16,112,2048]{2,1,0:T(8,128)(2,1)} fusion(bf16[16,256,2048]{2,1,0:T(8,128)(2,1)} %bitcast.188, s32[16,256]{1,0:T(8,128)S(1)} %convolution_convert_fusion.11, pred[16,256]{1,0:T(8,128)(4,1)S(1)} %compare_bitcast_fusion), kind=kOutput, calls=%fused_computation.12 | convolution fusion | flops 1883635712 | bytes 24137728 | tf_op jit(solution)/shard_map/sct,std->scd/dot_general | solution.py:928
  398.7 8.7 fusion.14
  407.5 19.5 %multiply_convert_fusion.5 = (bf16[1792,704]{0,1:T(8,128)(2,1)S(1)}, f32[1792,704]{0,1:T(8,128)}) fusion(f32[1792,704]{0,1:T(8,128)S(1)} %fusion.14, bf16[1792,2048]{1,0:T(8,128)(2,1)S(1)} %bitcast.218, bf16[1,2048,704]{1,2,0:T(8,128)(2,1)S(1)} %copy-done.92), kind=kOutput, calls=%fused_computation.9 | convolution fusion | flops 5174951936 | bytes 22839296 | tf_op jit(solution)/shard_map/dot_general | solution.py:939
  427.0 6.2 multiply_convert_fusion
  433.3 14.4 %spread_rows.2 = bf16[4096,2048]{1,0:T(8,128)(2,1)} custom-call(bf16[16,112,256]{2,1,0:T(8,128)(2,1)S(1)} %copy-done.5, bf16[16,112,2048]{2,1,0:T(8,128)(2,1)S(1)} %bitcast.193, bf16[4096,128]{1,0:T(8,128)(2,1)S(1)} %multiply_convert_fusion.9.units_ref, bf16[2048,128]{1,0:T(8,128)(2,1)S(1)} %slice.250.weight_ref), custom_call_target="tpu_custom_call" | custom-call | flops 4026531840 | bytes 24117248 | tf_op jit(solution)/shard_map/spread_rows/pallas_call | solution.py:767
  448.9 2.3 slice.247.weight_ref
  451.2 6.0 fusion.56
  457.2 5.2 convolution_convert_fusion.10
  464.6 5.9 multiply_convert_fusion.8
  470.6 6.1 convolution_convert_fusion.5
  478.3 12.2 %all-to-all-start.1 = ((bf16[16,384,128]{2,1,0:T(8,128)(2,1)}), bf16[16,384,128]{2,1,0:T(8,128)(2,1)}, u32[]{:S(2)}, u32[]{:S(2)}) async-start(bf16[16,384,128]{2,1,0:T(8,128)(2,1)} %bitcast_bitcast_fusion), calls=%async_computation.3 | async-start | bytes 3145728 | tf_op jit(solution)/shard_map/all_to_all | solution.py:983
  490.9 6.8 multiply_convert_fusion.2
  497.8 6.9 multiply_convert_fusion.1
  504.6 7.5 pad_maximum_fusion
  512.3 11.8 %multiply_convert_fusion.3 = (bf16[1792,704]{0,1:T(8,128)(2,1)S(1)}, bf16[1792,704]{0,1:T(8,128)(2,1)S(1)}) fusion(f32[1792,704]{0,1:T(8,128)} %copy-done.95, f32[1792,704]{0,1:T(8,128)} %get-tuple-element.202, bf16[1792,2048]{1,0:T(8,128)(2,1)} %bitcast.229, bf16[1,704,2048]{2,1,0:T(8,128)(2,1)S(1)} %copy-done), kind=kOutput, calls=%fused_computation.7 | convolution fusion | flops 5183782912 | bytes 25362432 | tf_op jit(solution)/shard_map/dot_general | solution.py:955
  524.1 9.1 fusion.12
  533.3 9.6 add_convert_fusion
  542.9 14.7 %spread_rows.3 = bf16[4096,2048]{1,0:T(8,128)(2,1)} custom-call(bf16[16,112,256]{2,1,0:T(8,128)(2,1)S(1)} %copy-done.6, bf16[16,112,2048]{2,1,0:T(8,128)(2,1)S(1)} %bitcast.192, bf16[4096,256]{1,0:T(8,128)(2,1)S(1)} %pad_maximum_fusion.1.units_ref, bf16[2048,256]{1,0:T(8,128)(2,1)S(1)} %copy-done.9), custom_call_target="tpu_custom_call" | custom-call | flops 6174015488 | bytes 24117248 | tf_op jit(solution)/shard_map/spread_rows/pallas_call | solution.py:767
  557.5 137.4 %reduce_rows.2 = f32[128,2048]{1,0:T(8,128)} custom-call(bf16[4,2,2,2,128,2048]{5,4,3,2,1,0:T(8,128)(2,1)} %bitcast.214), custom_call_target="tpu_custom_call" | custom-call | tf_op jit(solution)/shard_map/reduce_rows/pallas_call | solution.py:678
  696.7 2.7 fusion.92
  699.4 1.9 pair_rows.5
  701.4 2.1 convolution_convert_fusion.8
  704.8 1.8 fusion.52
  706.6 4.9 fusion.37
  713.3 5.0 fusion.34
  719.5 2.3 convolution_bitcast_fusion.3
  725.0 4.6 fusion.103
  729.7 3.2 pair_rows.6
  734.6 4.4 convolution_convert_fusion.2
  739.0 1.7 copy-done.13
  740.7 3.9 multiply_reduce_fusion.2
  746.2 2.8 copy.168
  749.0 6.2 convolution_convert_fusion
  755.2 10.7 %convolution_bitcast_fusion.2 = f32[1,704,2048]{2,1,0:T(8,128)} fusion(bf16[1792,704]{0,1:T(8,128)(2,1)S(1)} %copy-done.101, bf16[1792,2048]{1,0:T(8,128)(2,1)} %bitcast.230), kind=kOutput, calls=%fused_computation.19 | convolution fusion | flops 5167382528 | bytes 15630336 | tf_op jit(solution)/shard_map/dot_general | solution.py:972
  766.0 7.3 convolution_bitcast_fusion
  773.2 2.2 convolution_convert_fusion.4
  775.4 178.5 %reduce_rows.3 = (f32[128,1536]{1,0:T(8,128)}, f32[32,2048]{1,0:T(8,128)}, f32[64,576]{1,0:T(8,128)}, f32[16,384]{1,0:T(8,128)}) custom-call(bf16[4,2,2,128,1536]{4,3,2,1,0:T(8,128)(2,1)} %bitcast.215, bf16[4,2,2,32,2048]{4,3,2,1,0:T(8,128)(2,1)} %bitcast.223, bf16[4,2,2,2,64,576]{5,4,3,2,1,0:T(8,128)(2,1)} %bitcast.222, bf16[4,2,2,16,384]{4,3,2,1,0:T(8,128)(2,1)} %bitcast.246), custom_call_target="tpu_custom_call" | custom-call | tf_op jit(solution)/shard_map/reduce_rows/pallas_call | solution.py:678
  954.0 2.7 subtract_add_fusion.refs_1_
  956.6 10.2 %convolution_bitcast_fusion.1 = f32[1,2048,704]{1,2,0:T(8,128)} fusion(bf16[1792,704]{0,1:T(8,128)(2,1)S(1)} %copy-done.99, bf16[1792,2048]{1,0:T(8,128)(2,1)} %bitcast.217), kind=kOutput, calls=%fused_computation.18 | convolution fusion | flops 5167382528 | bytes 15630336 | tf_op jit(solution)/shard_map/dot_general | solution.py:973
  966.8 2.4 fusion.93
  969.3 2.4 copy.173
  974.1 3.8 pair_rows.7
  985.1 3.3 copy.207
  (323 shorter events, 67.8 us)
Async XLA Ops:
  7.2 419.8 %copy-start = (bf16[1,704,2048]{2,1,0:T(8,128)(2,1)S(1)}, bf16[1,704,2048]{2,1,0:T(8,128)(2,1)}, u32[]{:S(2)}) copy-start(bf16[1,704,2048]{2,1,0:T(8,128)(2,1)} %param.31) | copy-start | bytes 8650756
  7.2 216.1 %all-gather.3.cloned.1.call-start = ((), (), s32[]{:S(2)}) async-start(), calls=%async_computation.4 | async-start | bytes 8650752 | tf_op jit(solution)/shard_map/all_gather | solution.py:868
  145.4 6.1 copy-start.66
  145.4 46.9 %copy-start.68 = (f32[2048]{0:T(1024)}, f32[2048]{0:T(1024)S(1)}, u32[]{:S(2)}) copy-start(f32[2048]{0:T(1024)S(1)} %get-tuple-element.53) | copy-start | bytes 24580
  147.6 300.0 %all-gather.5.cloned.1.call-start = ((), (), s32[]{:S(2)}) async-start(), calls=%async_computation.5 | async-start | bytes 8650752 | tf_op jit(solution)/shard_map/all_gather | solution.py:868
  154.2 15.2 %copy-start.39 = (f32[256,576]{1,0:T(8,128)}, f32[256,576]{1,0:T(8,128)S(1)}, u32[]{:S(2)}) copy-start(f32[256,576]{1,0:T(8,128)S(1)} %fusion.99) | copy-start | bytes 1769476
  168.6 4.2 copy-start.77
  169.4 278.3 %copy-start.79 = (f32[256]{0:T(256)}, f32[256]{0:T(256)S(1)}, u32[]{:S(2)}) copy-start(f32[256]{0:T(256)S(1)} %add_rsqrt_fusion) | copy-start | bytes 3076
  172.7 8.2 copy-start.61
  172.7 8.2 copy-start.74
  175.0 5.8 copy-start.85
  176.1 8.0 copy-start.57
  192.3 118.1 %copy-start.83 = (f32[128]{0:T(128)}, f32[128]{0:T(128)S(1)}, u32[]{:S(2)}) copy-start(f32[128]{0:T(128)S(1)} %get-tuple-element.194) | copy-start | bytes 1540
  310.5 5.7 copy-start.2
  321.8 50.7 %all-to-all-start = ((bf16[16,128,384]{1,2,0:T(8,128)(2,1)}), bf16[16,128,384]{1,2,0:T(8,128)(2,1)}, u32[]{:S(2)}, u32[]{:S(2)}) async-start(bf16[16,128,384]{1,2,0:T(8,128)(2,1)} %fusion.33), calls=%async_computation | async-start | bytes 3145728 | tf_op jit(solution)/shard_map/all_to_all | solution.py:833
  326.2 412.8 %reduce-scatter.3.cloned.1.call-start = ((), (), s32[]{:S(2)}) async-start(), calls=%async_computation.6 | async-start | bytes 17301504 | tf_op jit(solution)/shard_map/reduce_scatter | solution.py:953
  387.1 46.1 %copy-start.3 = (bf16[4096,128]{1,0:T(8,128)(2,1)}, bf16[4096,128]{1,0:T(8,128)(2,1)S(1)}, u32[]{:S(2)}) copy-start(bf16[4096,128]{1,0:T(8,128)(2,1)S(1)} %multiply_convert_fusion.9.units_ref) | copy-start | bytes 3145732
  387.1 11.6 %copy-start.90 = (bf16[1,2048,704]{1,2,0:T(8,128)(2,1)S(1)}, bf16[1,2048,704]{1,2,0:T(8,128)(2,1)}, u32[]{:S(2)}) copy-start(bf16[1,2048,704]{1,2,0:T(8,128)(2,1)} %param.29) | copy-start | bytes 8650756
  398.7 8.7 copy-start.32
  398.7 8.7 copy-start.92
  407.5 19.5 %copy-start.95 = (f32[1792,704]{0,1:T(8,128)}, f32[1792,704]{0,1:T(8,128)S(1)}, u32[]{:S(2)}) copy-start(f32[1792,704]{0,1:T(8,128)S(1)} %fusion.14) | copy-start | bytes 15138820
  427.0 6.2 copy-start.100
  427.0 6.2 copy-start.5
  451.2 6.0 copy-start.4
  451.2 11.2 %slice-start.4 = ((s8[8388608]{0:T(1024)(128)(4,1)}), s8[4194304]{0:T(1024)(128)(4,1)S(1)}, s32[]{:S(2)}) async-start(s8[8388608]{0:T(1024)(128)(4,1)} %bitcast.212), calls=%async_computation.12 | async-start | bytes 8388608
  457.1 5.2 slice-start.5
  462.4 8.1 slice-start
  462.4 8.1 slice-start.1
  464.6 6.0 slice-start.2
  464.6 6.0 slice-start.3
  478.3 488.5 %all-to-all-start.1 = ((bf16[16,384,128]{2,1,0:T(8,128)(2,1)}), bf16[16,384,128]{2,1,0:T(8,128)(2,1)}, u32[]{:S(2)}, u32[]{:S(2)}) async-start(bf16[16,384,128]{2,1,0:T(8,128)(2,1)} %bitcast_bitcast_fusion), calls=%async_computation.3 | async-start | bytes 3145728 | tf_op jit(solution)/shard_map/all_to_all | solution.py:983
  490.5 482.3 %reduce-scatter.5.cloned.1.call-start = ((), (), s32[]{:S(2)}) async-start(), calls=%async_computation.7 | async-start | bytes 4456448 | tf_op jit(solution)/shard_map/reduce_scatter | solution.py:1001
  504.6 7.5 copy-start.52
  504.6 7.5 copy-start.53
  512.3 11.8 %copy-start.91 = (bf16[1,2048,704]{1,2,0:T(8,128)(2,1)S(1)}, bf16[1,2048,704]{1,2,0:T(8,128)(2,1)}, u32[]{:S(2)}) copy-start(bf16[1,2048,704]{1,2,0:T(8,128)(2,1)} %param.29) | copy-start | bytes 8650756
  524.1 9.1 copy-start.98
  524.1 9.1 copy-start.96
  524.1 9.1 copy-start.93
  533.3 9.6 copy-start.6
  533.3 9.6 copy-start.9
  557.5 137.4 %copy-start.30 = (f32[128,2048]{1,0:T(8,128)S(1)}, f32[128,2048]{1,0:T(8,128)}, u32[]{:S(2)}) copy-start(f32[128,2048]{1,0:T(8,128)} %copy-done.29) | copy-start | bytes 3145732
  557.5 137.4 %copy-start.69 = (f32[2048]{0:T(1024)S(1)}, f32[2048]{0:T(1024)}, u32[]{:S(2)}) copy-start(f32[2048]{0:T(1024)} %copy-done.68) | copy-start | bytes 24580
  557.5 137.5 %copy-start.84 = (f32[128]{0:T(128)S(1)}, f32[128]{0:T(128)}, u32[]{:S(2)}) copy-start(f32[128]{0:T(128)} %copy-done.83) | copy-start | bytes 1540
  696.7 4.7 copy-start.28
  701.4 3.4 copy-start.44
  729.6 3.4 copy-start.49
  729.6 3.4 copy-start.78
  733.0 6.0 copy-start.19
  740.7 4.7 copy-start.38
  749.0 6.2 copy-start.101
  749.0 16.9 %slice-start.6 = ((s8[7340032]{0:T(1024)(128)(4,1)}), s8[3145728]{0:T(1024)(128)(4,1)S(1)}, s32[]{:S(2)}) async-start(s8[7340032]{0:T(1024)(128)(4,1)} %bitcast.219), calls=%async_computation.14 | async-start | bytes 6291456
  755.2 10.7 %slice-start.7 = ((s8[7340032]{0:T(1024)(128)(4,1)}), s8[4194304]{0:T(1024)(128)(4,1)S(1)}, s32[]{:S(2)}) async-start(s8[7340032]{0:T(1024)(128)(4,1)} %bitcast.219), calls=%async_computation.15 | async-start | bytes 8388608
  755.2 10.7 %copy-start.97 = (bf16[1792,704]{0,1:T(8,128)(2,1)S(1)}, bf16[1792,704]{0,1:T(8,128)(2,1)}, u32[]{:S(2)}) copy-start(bf16[1792,704]{0,1:T(8,128)(2,1)} %copy-done.96) | copy-start | bytes 7569412
  765.9 7.3 copy-start.40
  765.9 7.3 copy-start.46
  766.0 7.3 copy-start.80
  775.4 178.5 %copy-start.34 = (f32[256,2048]{1,0:T(8,128)S(1)}, f32[256,2048]{1,0:T(8,128)}, u32[]{:S(2)}) copy-start(f32[256,2048]{1,0:T(8,128)} %convert_element_type.160) | copy-start | bytes 6291460
  775.4 178.5 %copy-start.47 = (f32[128,2048]{1,0:T(8,128)S(1)}, f32[128,2048]{1,0:T(8,128)}, u32[]{:S(2)}) copy-start(f32[128,2048]{1,0:T(8,128)} %get-tuple-element.152) | copy-start | bytes 3145732
  775.4 178.5 %copy-start.88 = (f32[128]{0:T(128)S(1)}, f32[128]{0:T(128)}, u32[]{:S(2)}) copy-start(f32[128]{0:T(128)} %get-tuple-element.204) | copy-start | bytes 1540
  969.3 3.5 copy-start.31
  969.3 3.5 copy-start.60
  980.2 3.9 copy-start.18
  985.1 4.2 copy-start.65
  985.1 4.9 copy-start.1
  (52 other events, 102.2 us)
Sparse Core Ops, SparseCore 0:
  147.7 75.5 all-gather.2
  316.3 96.4 all-gather.4
  447.8 263.4 reduce-scatter.2
  739.1 136.5 reduce-scatter.4

commit v4 on v3

--- a/solution.py
+++ b/solution.py
@@ -869,7 +869,8 @@
 
     cot_half = rows_of(cotangent, core)
     cot_bf = cot_half.astype(bf16)
-    cot_left, gain_two = all_rows(cot_bf[:, : width // 2], gain_two)
+    left = width * 3 // 8 // 128 * 128
+    cot_left, gain_two = all_rows(cot_bf[:, :left], gain_two)
 
     cosine, sine = rope_tables(length)
     scale = (NOPE + ROPE) ** (-0.5)
@@ -915,7 +916,7 @@
     ffn_in, cot_left = lax.optimization_barrier((ffn_in, cot_left))
     (ffn_all,) = gather(grid, [ffn_in], [True], cut(0, half, GATHER_ORDERS, core_last=True), 2)
     ffn_all = ffn_all.reshape(-1, width)
-    cot_right, ffn_all = all_rows(cot_bf[:, width // 2 :], ffn_all)
+    cot_right, ffn_all = all_rows(cot_bf[:, left:], ffn_all)
 
     routed = gates > 0.0
     triangle = (position[:, None] < position[None, :]).astype(bf16)
@@ -960,8 +961,8 @@
     back_part = lax.dot_general(
         gate_gradient, local_gate, (((1,), (1,)), ((), ())), preferred_element_type=f32
     ) + lax.dot_general(up_gradient, local_up, (((1,), (1,)), ((), ())), preferred_element_type=f32)
-    shared_hg = jnp.dot(cot_left, s_down_t[: width // 2], preferred_element_type=f32) + jnp.dot(
-        cot_right, s_down_t[width // 2 :], preferred_element_type=f32
+    shared_hg = jnp.dot(cot_left, s_down_t[:left], preferred_element_type=f32) + jnp.dot(
+        cot_right, s_down_t[left:], preferred_element_type=f32
     )
     grad_units = jnp.concatenate(
         [shared_hg * shared_u * silu_slope(shared_g), shared_hg * jax.nn.silu(shared_g)], axis=1
@@ -997,8 +998,6 @@
     (grad_attn,) = pair(grid, [grad_residual.astype(bf16)], True, 6)
     grad_attn = grad_attn.reshape(length, width)
     g_out_t = jnp.dot(grad_attn.T, context, preferred_element_type=f32)
-    g_out_t, ffn_total = lax.optimization_barrier((g_out_t.astype(bf16), ffn_total))
-    s_out_t = lax.psum_scatter(g_out_t, "dp", scatter_dimension=0, tiled=True)
     grad_context = (
         jnp.dot(grad_attn, full_out_t, preferred_element_type=f32)
         .astype(bf16)
@@ -1061,21 +1060,22 @@
     g_gains = jnp.pad(g_gains[:, None, :], ((0, 0), (0, 15), (0, 0)))
     terms = [
         g_query.astype(bf16).reshape(grid + (-1, g_query.shape[1])),
+        g_out_t.astype(bf16).reshape(grid + (-1, g_out_t.shape[1])),
         g_up.astype(bf16).reshape(grid + (-1, g_up.shape[1])),
         g_latent.astype(bf16).reshape(grid + (2, -1, g_latent.shape[1])),
         g_gains.astype(bf16).reshape(grid + (16, -1)),
     ]
     pieces = (
         cut(0, terms[0].shape[-2], REDUCE_ORDERS)
-        + cut(1, terms[1].shape[-2], ((1, (X, Y, Z)), (1, (Y, X, Z))))
-        + cut(2, terms[2].shape[-2], ((1, (Z, X, Y)),), core_first=True)
-        + cut(3, terms[3].shape[-2], ((1, (X, Y, Z)),))
-    )
-    s_query, s_up, latent_half, gain_sums = reduce(
-        grid, terms, [False, False, True, False], pieces, 4
-    )
-    ffn_total, s_out_t, gain_sums = lax.optimization_barrier((ffn_total, s_out_t, gain_sums))
-    s_out_t = s_out_t.astype(f32)
+        + cut(1, terms[1].shape[-2], REDUCE_ORDERS)
+        + cut(2, terms[2].shape[-2], ((1, (X, Y, Z)), (1, (Y, X, Z))))
+        + cut(3, terms[3].shape[-2], ((1, (Z, X, Y)),), core_first=True)
+        + cut(4, terms[4].shape[-2], ((1, (X, Y, Z)),))
+    )
+    s_query, s_out_t, s_up, latent_half, gain_sums = reduce(
+        grid, terms, [False, False, False, True, False], pieces, 4
+    )
+    ffn_total, gain_sums = lax.optimization_barrier((ffn_total, gain_sums))
     output_half = (residual + ffn_total.astype(f32)).astype(bf16)
     output, grad_input, s_latent, gain_sums = pair(
         grid, [output_half, grad_input_half, latent_half, gain_sums], True, 8

time: 1010 us -> 990 us (0.980)
    unnamed x237 -> x239, local copies, waits for them, and re-layouts: 47.5 us -> 43.3 us
  transfers between devices with their start and end apart: 6 -> 5, of which waited for: 2 -> 2; matrix products, arithmetic and copies ran while one was open for 28% -> 28% of each run, Pallas kernels for 35% -> 35%
where the time goes in v4:
time: 990 us; the launch traced here: 980 us
  Pallas kernels  561 us (57%)
  matrix products  201 us (20%)
  local copies, waits for them, and re-layouts  81.1 us (8%)
  waiting for transfers between devices  67 us (7%)
  other arithmetic  36.1 us (4%)
  starting transfers between devices  18.8 us (2%)
  between operations  15.7 us (2%)
    pallas_call x2, Pallas kernels, reduce(): pl.pallas_call(functools.partial(reduce_body, grid, pieces, shared_flags,...  309 us
    pallas_call x2, Pallas kernels, gather(): pl.pallas_call(functools.partial(gather_body, grid, pieces, shared_flags,...  210 us
    all_to_all x1, waiting for transfers between devices, dense_shards(): lax.all_to_all(stacked, 'dp', split_axis=0, concat_axis=0, tiled=True)  45.8 us
    unnamed x239, local copies, waits for them, and re-layouts  43.3 us
    pallas_call x2, Pallas kernels, spread_rows(): pl.pallas_call(spread_body, grid=(count,), out_shape=jax.ShapeDtypeStruct...  29 us
    dot_general x3, matrix products, take(): jnp.einsum('sct,std->scd', pick, rows.reshape(chips, length, -1), preferr...  23.2 us
    all_gather x2, waiting for transfers between devices, all_rows(): return (lax.all_gather(part, ('dp', 'tensor'), axis=0, tiled=True), after)  21.1 us
  transfers between devices with their start and end apart: 5, of which 2 were waited for; matrix products, arithmetic and copies ran while one was open for 28% of the time, Pallas kernels for 35%

profile of v4, /device:TPU:0, one launch (start us, length us, event | category | flops | bytes accessed | tf_op | source)
XLA Modules:
  0.0 980.4 jit_solution(18255819135469748367)
XLA Ops:
  14.0 123.0 %gather_rows.2 = (bf16[4,2,2,128,1536]{4,3,2,1,0:T(8,128)(2,1)S(1)}, bf16[4,2,2,128,1024]{4,3,2,1,0:T(8,128)(2,1)S(1)}, bf16[4,2,2,32,2048]{4,3,2,1,0:T(8,128)(2...) custom-call(bf16[128,1536]{1,0:T(8,128)(2,1)S(1)} %copy-done.18, ...), custom_call_target="tpu_custom_call" | custom-call | tf_op jit(solution)/shard_map/gather_rows/pallas_call | solution.py:500
  140.7 2.6 copy-done.23
  143.3 2.0 copy-done.24
  148.8 2.9 convert_element_type.159
  159.3 6.1 fusion.99
  165.3 3.0 copy.142
  170.0 3.3 convolution_convert_fusion.6
  173.3 2.3 copy.184
  179.3 2.1 slice.324
  182.8 1.9 fusion.31
  186.0 1.8 copy-done.25
  189.3 3.3 pair_rows.4
  194.1 21.1 %all-gather.3.cloned.1.call-done = bf16[4096,768]{1,0:T(8,128)(2,1)} async-done(((bf16[128,768]{1,0:T(8,128)(2,1)}), bf16[4096,768]{1,0:T(8,128)(2,1)}) %all-gather.3.cloned.1.call-update) | async-done | bytes 6291472 | tf_op jit(solution)/shard_map/all_gather | solution.py:868
  215.2 87.1 %gather_rows.3 = bf16[4,2,2,2,128,2048]{5,4,3,2,1,0:T(8,128)(2,1)S(1)} custom-call(bf16[128,2048]{1,0:T(8,128)(2,1)S(1)} %multiply_convert_fusion.11.refs_0_), custom_call_target="tpu_custom_call" | custom-call | tf_op jit(solution)/shard_map/gather_rows/pallas_call | solution.py:500
  302.4 5.7 copy-done.2
  309.3 1.9 copy.153
  311.2 2.5 fusion.33
  313.7 4.4 all-to-all-start
  321.1 45.8 %all-to-all-done = bf16[16,128,384]{1,2,0:T(8,128)(2,1)} async-done(((bf16[16,128,384]{1,2,0:T(8,128)(2,1)}), bf16[16,128,384]{1,2,0:T(8,128)(2,1)}, u32[]{:S(2)}, u32[]{:S(2)}) %all-to-all-start) | async-done | bytes 1572896 | tf_op jit(solution)/shard_map/all_to_all | solution.py:833
  366.9 2.7 copy.154
  370.6 8.9 fusion.90
  381.8 11.6 %convolution_convert_fusion.1 = bf16[16,112,2048]{2,1,0:T(8,128)(2,1)} fusion(bf16[16,256,2048]{2,1,0:T(8,128)(2,1)} %bitcast.188, s32[16,256]{1,0:T(8,128)S(1)} %convolution_convert_fusion.11, pred[16,256]{1,0:T(8,128)(4,1)S(1)} %compare_bitcast_fusion), kind=kOutput, calls=%fused_computation.12 | convolution fusion | flops 1883635712 | bytes 24137728 | tf_op jit(solution)/shard_map/sct,std->scd/dot_general | solution.py:929
  393.4 8.6 fusion.14
  402.1 19.3 %multiply_convert_fusion.5 = (bf16[1792,704]{0,1:T(8,128)(2,1)S(1)}, f32[1792,704]{0,1:T(8,128)}) fusion(f32[1792,704]{0,1:T(8,128)S(1)} %fusion.14, bf16[1792,2048]{1,0:T(8,128)(2,1)S(1)} %bitcast.221, bf16[1,2048,704]{1,2,0:T(8,128)(2,1)S(1)} %copy-done.88), kind=kOutput, calls=%fused_computation.9 | convolution fusion | flops 5174951936 | bytes 22839296 | tf_op jit(solution)/shard_map/dot_general | solution.py:940
  421.4 6.2 multiply_convert_fusion
  427.6 14.4 %spread_rows.2 = bf16[4096,2048]{1,0:T(8,128)(2,1)} custom-call(bf16[16,112,256]{2,1,0:T(8,128)(2,1)S(1)} %copy-done.5, bf16[16,112,2048]{2,1,0:T(8,128)(2,1)S(1)} %bitcast.193, bf16[4096,128]{1,0:T(8,128)(2,1)S(1)} %multiply_convert_fusion.9.units_ref, bf16[2048,128]{1,0:T(8,128)(2,1)S(1)} %slice.250.weight_ref), custom_call_target="tpu_custom_call" | custom-call | flops 4026531840 | bytes 24117248 | tf_op jit(solution)/shard_map/spread_rows/pallas_call | solution.py:767
  443.3 2.3 slice.247.weight_ref
  445.6 4.0 convolution_convert_fusion.10
  449.6 5.9 convolution_convert_fusion.7
  455.8 4.0 fusion.55
  459.9 5.8 multiply_convert_fusion.8
  465.7 6.1 convolution_convert_fusion.5
  473.4 14.2 %all-to-all-start.1 = ((bf16[16,384,128]{2,1,0:T(8,128)(2,1)}), bf16[16,384,128]{2,1,0:T(8,128)(2,1)}, u32[]{:S(2)}, u32[]{:S(2)}) async-start(bf16[16,384,128]{2,1,0:T(8,128)(2,1)} %bitcast_bitcast_fusion), calls=%async_computation.2 | async-start | bytes 3145728 | tf_op jit(solution)/shard_map/all_to_all | solution.py:984
  487.7 3.9 multiply_convert_fusion.2
  491.6 7.8 multiply_convert_fusion.1
  499.4 6.7 pad_maximum_fusion
  507.5 11.7 %multiply_convert_fusion.3 = (bf16[1792,704]{0,1:T(8,128)(2,1)S(1)}, bf16[1792,704]{0,1:T(8,128)(2,1)S(1)}) fusion(f32[1792,704]{0,1:T(8,128)} %copy-done.91, f32[1792,704]{0,1:T(8,128)} %get-tuple-element.196, bf16[1792,2048]{1,0:T(8,128)(2,1)} %bitcast.232, bf16[1,704,2048]{2,1,0:T(8,128)(2,1)S(1)} %copy-done), kind=kOutput, calls=%fused_computation.7 | convolution fusion | flops 5183782912 | bytes 25362432 | tf_op jit(solution)/shard_map/dot_general | solution.py:956
  519.3 9.3 fusion.12
  528.6 10.0 %add_convert_fusion = bf16[1792,2048]{1,0:T(8,128)(2,1)S(1)} fusion(f32[1792,2048]{1,0:T(8,128)} %fusion.12, bf16[1792,704]{0,1:T(8,128)(2,1)S(1)} %get-tuple-element.151, bf16[1,2048,704]{1,2,0:T(8,128)(2,1)S(1)} %copy-done.89), kind=kOutput, calls=%fused_computation.1 | convolution fusion | flops 5174722560 | bytes 27426816 | tf_op jit(solution)/shard_map/dot_general | solution.py:963
  538.6 14.7 %spread_rows.3 = bf16[4096,2048]{1,0:T(8,128)(2,1)} custom-call(bf16[16,112,256]{2,1,0:T(8,128)(2,1)S(1)} %copy-done.6, bf16[16,112,2048]{2,1,0:T(8,128)(2,1)S(1)} %bitcast.192, bf16[4096,256]{1,0:T(8,128)(2,1)S(1)} %pad_maximum_fusion.1.units_ref, bf16[2048,256]{1,0:T(8,128)(2,1)S(1)} %copy-done.9), custom_call_target="tpu_custom_call" | custom-call | flops 6174015488 | bytes 24117248 | tf_op jit(solution)/shard_map/spread_rows/pallas_call | solution.py:767
  553.3 138.3 %reduce_rows.2 = f32[128,2048]{1,0:T(8,128)} custom-call(bf16[4,2,2,2,128,2048]{5,4,3,2,1,0:T(8,128)(2,1)} %bitcast.213), custom_call_target="tpu_custom_call" | custom-call | tf_op jit(solution)/shard_map/reduce_rows/pallas_call | solution.py:678
  693.3 2.7 fusion.92
  696.0 2.0 pair_rows.5
  698.1 2.1 convolution_convert_fusion.9
  703.4 4.9 fusion.37
  710.0 5.0 fusion.34
  716.2 2.3 convolution_bitcast_fusion.3
  720.9 4.9 fusion.102
  725.9 3.2 pair_rows.6
  729.7 4.4 multiply_reduce_fusion.2
  734.8 2.2 convolution_convert_fusion.3
  737.1 4.6 copy.168
  741.8 3.3 convolution_convert_fusion.2
  745.1 4.8 convolution_convert_fusion
  749.9 7.1 convolution_bitcast_fusion.2
  757.1 7.3 convolution_bitcast_fusion
  764.4 2.2 convolution_convert_fusion.4
  766.6 171.0 %reduce_rows.3 = (f32[128,1536]{1,0:T(8,128)}, f32[128,1024]{1,0:T(8,128)}, f32[32,2048]{1,0:T(8,128)}, f32[64,576]{1,0:T(8,128)}, f32[16,384]{1,0:T(8,128)}) custom-call(bf16[4,2,2,128,1536]{4,3,2,1,0:T(8,128)(2,1)} %bitcast.214, bf16[4,2,2,128,1024]{4,3,2,1,0:T(8,128)(2,1)} %bitcast.215, bf16[4,2,2,32,2048]{4,3,2,1,0:T(8,128)(2,1)} %bitcast.226, ...), custom_call_target="tpu_custom_call" | custom-call | tf_op jit(solution)/shard_map/reduce_rows/pallas_call | solution.py:678
  937.5 2.0 copy.172
  939.6 3.0 subtract_add_fusion.refs_1_
  942.6 10.2 %convolution_bitcast_fusion.1 = f32[1,2048,704]{1,2,0:T(8,128)} fusion(bf16[1792,704]{0,1:T(8,128)(2,1)S(1)} %copy-done.95, bf16[1792,2048]{1,0:T(8,128)(2,1)} %bitcast.220), kind=kOutput, calls=%fused_computation.18 | convolution fusion | flops 5167382528 | bytes 15630336 | tf_op jit(solution)/shard_map/dot_general | solution.py:974
  952.8 2.2 fusion.93
  959.7 3.8 pair_rows.7
  967.7 2.5 copy.206
  (324 shorter events, 67.6 us)
Async XLA Ops:
  7.2 414.2 %copy-start = (bf16[1,704,2048]{2,1,0:T(8,128)(2,1)S(1)}, bf16[1,704,2048]{2,1,0:T(8,128)(2,1)}, u32[]{:S(2)}) copy-start(bf16[1,704,2048]{2,1,0:T(8,128)(2,1)} %param.31) | copy-start | bytes 8650756
  7.2 208.0 %all-gather.3.cloned.1.call-start = ((), (), s32[]{:S(2)}) async-start(), calls=%async_computation.3 | async-start | bytes 6488064 | tf_op jit(solution)/shard_map/all_gather | solution.py:868
  145.3 6.7 copy-start.62
  145.3 48.2 %copy-start.64 = (f32[2048]{0:T(1024)}, f32[2048]{0:T(1024)S(1)}, u32[]{:S(2)}) copy-start(f32[2048]{0:T(1024)S(1)} %get-tuple-element.52) | copy-start | bytes 24580
  147.4 294.6 %all-gather.5.cloned.1.call-start = ((), (), s32[]{:S(2)}) async-start(), calls=%async_computation.4 | async-start | bytes 10813440 | tf_op jit(solution)/shard_map/all_gather | solution.py:868
  154.8 15.2 %copy-start.37 = (f32[256,576]{1,0:T(8,128)}, f32[256,576]{1,0:T(8,128)S(1)}, u32[]{:S(2)}) copy-start(f32[256,576]{1,0:T(8,128)S(1)} %fusion.98) | copy-start | bytes 1769476
  169.1 4.2 copy-start.73
  170.0 272.1 %copy-start.75 = (f32[256]{0:T(256)}, f32[256]{0:T(256)S(1)}, u32[]{:S(2)}) copy-start(f32[256]{0:T(256)S(1)} %add_rsqrt_fusion) | copy-start | bytes 3076
  173.3 8.2 copy-start.57
  173.3 8.2 copy-start.70
  175.6 5.8 copy-start.81
  176.7 8.0 copy-start.54
  193.5 108.8 %copy-start.79 = (f32[128]{0:T(128)}, f32[128]{0:T(128)S(1)}, u32[]{:S(2)}) copy-start(f32[128]{0:T(128)S(1)} %get-tuple-element.188) | copy-start | bytes 1540
  302.4 5.8 copy-start.2
  313.7 53.2 %all-to-all-start = ((bf16[16,128,384]{1,2,0:T(8,128)(2,1)}), bf16[16,128,384]{1,2,0:T(8,128)(2,1)}, u32[]{:S(2)}, u32[]{:S(2)}) async-start(bf16[16,128,384]{1,2,0:T(8,128)(2,1)} %fusion.33), calls=%async_computation | async-start | bytes 3145728 | tf_op jit(solution)/shard_map/all_to_all | solution.py:833
  318.1 639.2 %reduce-scatter.2.cloned.1.call-start = ((), (), s32[]{:S(2)}) async-start(), calls=%async_computation.5 | async-start | bytes 17301504 | tf_op jit(solution)/shard_map/reduce_scatter | solution.py:954
  381.8 45.8 %copy-start.3 = (bf16[4096,128]{1,0:T(8,128)(2,1)}, bf16[4096,128]{1,0:T(8,128)(2,1)S(1)}, u32[]{:S(2)}) copy-start(bf16[4096,128]{1,0:T(8,128)(2,1)S(1)} %multiply_convert_fusion.9.units_ref) | copy-start | bytes 3145732
  381.8 11.6 %copy-start.86 = (bf16[1,2048,704]{1,2,0:T(8,128)(2,1)S(1)}, bf16[1,2048,704]{1,2,0:T(8,128)(2,1)}, u32[]{:S(2)}) copy-start(bf16[1,2048,704]{1,2,0:T(8,128)(2,1)} %param.29) | copy-start | bytes 8650756
  393.4 8.6 copy-start.30
  393.4 8.7 copy-start.88
  402.1 19.3 %copy-start.91 = (f32[1792,704]{0,1:T(8,128)}, f32[1792,704]{0,1:T(8,128)S(1)}, u32[]{:S(2)}) copy-start(f32[1792,704]{0,1:T(8,128)S(1)} %fusion.14) | copy-start | bytes 15138820
  421.4 6.2 copy-start.96
  421.4 6.2 copy-start.5
  442.0 3.5 copy-start.4
  445.6 9.9 %slice-start.4 = ((s8[10485760]{0:T(1024)(128)(4,1)}), s8[4194304]{0:T(1024)(128)(4,1)S(1)}, s32[]{:S(2)}) async-start(s8[10485760]{0:T(1024)(128)(4,1)} %bitcast.211), calls=%async_computation.10 | async-start | bytes 8388608
  445.6 14.3 %slice-start.7 = ((s8[6291456]{0:T(1024)(128)(4,1)}), s8[4194304]{0:T(1024)(128)(4,1)S(1)}, s32[]{:S(2)}) async-start(s8[6291456]{0:T(1024)(128)(4,1)} %bitcast.217), calls=%async_computation.13 | async-start | bytes 8388608
  449.6 5.9 slice-start.5
  449.6 6.3 slice-start.6
  449.6 10.3 %slice-start.8 = ((s8[6291456]{0:T(1024)(128)(4,1)}), s8[2097152]{0:T(1024)(128)(4,1)S(1)}, s32[]{:S(2)}) async-start(s8[6291456]{0:T(1024)(128)(4,1)} %bitcast.217), calls=%async_computation.14 | async-start | bytes 4194304
  455.8 9.9 %slice-start = ((s8[16777216]{0:T(1024)(128)(4,1)}), s8[4194304]{0:T(1024)(128)(4,1)S(1)}, s32[]{:S(2)}) async-start(s8[16777216]{0:T(1024)(128)(4,1)} %bitcast.189), calls=%async_computation.6 | async-start | bytes 8388608
  455.8 9.9 %slice-start.1 = ((s8[16777216]{0:T(1024)(128)(4,1)}), s8[4194304]{0:T(1024)(128)(4,1)S(1)}, s32[]{:S(2)}) async-start(s8[16777216]{0:T(1024)(128)(4,1)} %bitcast.189), calls=%async_computation.7 | async-start | bytes 8388608
  459.9 5.8 slice-start.2
  459.9 5.8 slice-start.3
  473.4 479.4 %all-to-all-start.1 = ((bf16[16,384,128]{2,1,0:T(8,128)(2,1)}), bf16[16,384,128]{2,1,0:T(8,128)(2,1)}, u32[]{:S(2)}, u32[]{:S(2)}) async-start(bf16[16,384,128]{2,1,0:T(8,128)(2,1)} %bitcast_bitcast_fusion), calls=%async_computation.2 | async-start | bytes 3145728 | tf_op jit(solution)/shard_map/all_to_all | solution.py:984
  499.4 6.7 copy-start.49
  507.5 11.8 %copy-start.87 = (bf16[1,2048,704]{1,2,0:T(8,128)(2,1)S(1)}, bf16[1,2048,704]{1,2,0:T(8,128)(2,1)}, u32[]{:S(2)}) copy-start(bf16[1,2048,704]{1,2,0:T(8,128)(2,1)} %param.29) | copy-start | bytes 8650756
  519.2 9.3 copy-start.94
  519.2 9.3 copy-start.92
  519.3 9.3 copy-start.89
  528.5 10.1 %copy-start.6 = (bf16[16,112,256]{2,1,0:T(8,128)(2,1)S(1)}, bf16[16,112,256]{2,1,0:T(8,128)(2,1)}, u32[]{:S(2)}) copy-start(bf16[16,112,256]{2,1,0:T(8,128)(2,1)} %fusion.24.pick_ref) | copy-start | bytes 2752516
  528.6 10.1 %copy-start.9 = (bf16[2048,256]{1,0:T(8,128)(2,1)S(1)}, bf16[2048,256]{1,0:T(8,128)(2,1)}, u32[]{:S(2)}) copy-start(bf16[2048,256]{1,0:T(8,128)(2,1)} %slice.247.weight_ref) | copy-start | bytes 3145732
  553.3 138.3 %copy-start.28 = (f32[128,2048]{1,0:T(8,128)S(1)}, f32[128,2048]{1,0:T(8,128)}, u32[]{:S(2)}) copy-start(f32[128,2048]{1,0:T(8,128)} %copy-done.27) | copy-start | bytes 3145732
  553.3 138.3 %copy-start.65 = (f32[2048]{0:T(1024)S(1)}, f32[2048]{0:T(1024)}, u32[]{:S(2)}) copy-start(f32[2048]{0:T(1024)} %copy-done.64) | copy-start | bytes 24580
  553.3 138.3 %copy-start.80 = (f32[128]{0:T(128)S(1)}, f32[128]{0:T(128)}, u32[]{:S(2)}) copy-start(f32[128]{0:T(128)} %copy-done.79) | copy-start | bytes 1540
  693.3 4.8 copy-start.26
  698.1 3.4 copy-start.41
  720.9 4.9 copy-start.44
  725.8 3.4 copy-start.46
  725.8 3.4 copy-start.74
  725.9 3.7 copy-start.63
  729.7 5.2 copy-start.36
  737.1 4.7 copy-start.8
  737.1 4.7 copy-start.53
  741.7 8.2 slice-start.11
  745.1 4.8 slice-start.12
  745.1 4.8 copy-start.97
  745.1 12.0 %slice-start.9 = ((s8[7340032]{0:T(1024)(128)(4,1)}), s8[3145728]{0:T(1024)(128)(4,1)S(1)}, s32[]{:S(2)}) async-start(s8[7340032]{0:T(1024)(128)(4,1)} %bitcast.222), calls=%async_computation.15 | async-start | bytes 6291456
  749.9 7.2 slice-start.10
  749.9 7.2 copy-start.93
  757.1 7.3 copy-start.38
  757.1 7.3 copy-start.43
  757.1 7.3 copy-start.76
  766.6 173.0 %copy-start.32 = (f32[256,2048]{1,0:T(8,128)S(1)}, f32[256,2048]{1,0:T(8,128)}, u32[]{:S(2)}) copy-start(f32[256,2048]{1,0:T(8,128)} %convert_element_type.159) | copy-start | bytes 6291460
  766.6 173.0 %copy-start.84 = (f32[128]{0:T(128)S(1)}, f32[128]{0:T(128)}, u32[]{:S(2)}) copy-start(f32[128]{0:T(128)} %get-tuple-element.198) | copy-start | bytes 1540
  (52 other events, 109.6 us)
Sparse Core Ops, SparseCore 0:
  147.5 67.6 all-gather.2
  308.2 107.0 all-gather.4
  442.2 265.5 reduce-scatter.1
